TPU v7x, 256 devices: a whole 4x4x8 slice. The times are simulated.
256 devices in a mesh: depth: 8 (over z), col: 4 (over y), row: 8 (over x, core).
Axes of the slice: x: 4, y: 4, z: 8, core: 2. Of those that a mesh axis runs over, the one named last changes fastest.
Arguments:
- a_mat: bfloat16 [16384, 16384], P(('row', 'depth'), 'col')
- b_mat: bfloat16 [16384, 16384], P(('row', 'depth'), 'col')
Outputs:
- output: bfloat16 [16384, 16384], P(('row', 'depth'), 'col')
All inputs are finite; a program needn't handle non-finite values.
Results may differ from a plain program's by a relative error of at most 0.001.
Values are sent between devices in bfloat16 or wider.
A program may use at most 768 MiB of HBM per device.

v0:
```python
import jax
import jax.numpy as jnp
from jax import lax
from jax.sharding import PartitionSpec as P, NamedSharding


def solution(mesh):
    depth_n = mesh.shape["depth"]
    col_n = mesh.shape["col"]
    row_n = mesh.shape["row"]
    row_ratio = row_n // col_n
    layer_steps = row_n // depth_n
    all_axes = ("depth", "col", "row")

    def linear(layer, col_idx, row_idx):
        return (layer * col_n + col_idx) * row_n + row_idx

    def first_k(layer, row_idx):
        return (row_idx + layer * layer_steps) % row_n

    b_start = [
        (linear(layer, col_idx, (first_k(layer, row_idx) + col_idx * row_ratio) % row_n), linear(layer, col_idx, row_idx))
        for layer in range(depth_n) for col_idx in range(col_n) for row_idx in range(row_n)
    ]
    a_start = [
        (linear(layer, (col_idx + first_k(layer, row_idx) // row_ratio) % col_n, row_idx), linear(layer, col_idx, row_idx))
        for layer in range(depth_n) for col_idx in range(col_n) for row_idx in range(row_n)
    ]
    a_after = [
        (linear(layer, (col_idx + first_k(layer, row_idx) // row_ratio + 1) % col_n, row_idx), linear(layer, col_idx, row_idx))
        for layer in range(depth_n) for col_idx in range(col_n) for row_idx in range(row_n)
    ]
    b_shift = [((row_idx + 1) % row_n, row_idx) for row_idx in range(row_n)]
    a_shift = [((col_idx + 1) % col_n, col_idx) for col_idx in range(col_n)]

    def local_product(a_blk, b_blk):
        a_full = lax.all_gather(a_blk, "depth", axis=0, tiled=True)
        b_full = lax.all_gather(b_blk, "depth", axis=0, tiled=True)
        piece_w = a_full.shape[0]
        col_w = a_full.shape[1]
        b_cur = lax.ppermute(b_full, all_axes, b_start)
        a_lead = lax.ppermute(a_full, all_axes, a_start)
        if row_ratio == 1:
            queue = a_lead
        else:
            a_tail = lax.ppermute(a_full, all_axes, a_after)
            offset = (lax.axis_index("row") + lax.axis_index("depth") * layer_steps) % row_n % row_ratio
            joined = jnp.concatenate([a_lead, a_tail], axis=1)
            queue = lax.dynamic_slice_in_dim(joined, offset * piece_w, col_w, axis=1)
        pieces = [queue[:, slot * piece_w:(slot + 1) * piece_w] for slot in range(min(row_ratio, layer_steps))]
        part_sum = jnp.dot(pieces[0], b_cur, preferred_element_type=jnp.float32)
        for step in range(1, layer_steps):
            if step - 1 + row_ratio < layer_steps:
                pieces = pieces[1:] + [lax.ppermute(pieces[0], "col", a_shift)]
            else:
                pieces = pieces[1:]
            b_cur = lax.ppermute(b_cur, "row", b_shift)
            part_sum = part_sum + jnp.dot(pieces[0], b_cur, preferred_element_type=jnp.float32)
        c_part = lax.psum_scatter(part_sum, "depth", scatter_dimension=0, tiled=True)
        return c_part.astype(jnp.bfloat16)

    block_spec = P(("row", "depth"), "col")
    return jax.shard_map(local_product, mesh=mesh, in_specs=(block_spec, block_spec), out_specs=block_spec, check_vma=False)
```

profile of v0, /device:TPU:1, one launch (start us, length us, event | category | flops | bytes accessed | tf_op | source)
XLA Modules:
  0.0 1468.2 jit_solution(16492282688648974322)
XLA Ops:
  6.5 0.0 all-gather.5.cloned.1.call-start
  6.5 0.7 all-gather.5.cloned.1.call-update
  7.3 0.0 all-gather.3.cloned.1.call-start
  7.3 0.7 all-gather.3.cloned.1.call-update
  8.0 0.0 reduce-scatter.2.cloned.1.call-start
  8.1 177.3 %all-gather.5.cloned.1.call-done = bf16[2048,4096]{1,0:T(8,128)(2,1)} async-done(((bf16[256,4096]{1,0:T(8,128)(2,1)}), bf16[2048,4096]{1,0:T(8,128)(2,1)}) %all-gather.5.cloned.1.call-update) | async-done | bytes 16777232 | tf_op jit(solution)/shard_map/all_gather | solution.py:38
  185.3 126.8 %collective-permute-start.2 = (bf16[2048,4096]{1,0:T(8,128)(2,1)}, bf16[2048,4096]{1,0:T(8,128)(2,1)}, u32[]{:S(2)}, u32[]{:S(2)}) collective-permute-start(bf16[2048,4096]{1,0:T(8,128)(2,1)} %all-gather.5.cloned.1.call-done), channel_id=1, source_target_pairs={{0,0},{1,1},{2,2},{3,3},{4,4},{5,5},{6,6},{7,7},{10,8},{11,9},{12,... | collective-permute-start | bytes 50331656 | tf_op jit(solution)/shard_map/ppermute | solution.py:41
  312.1 46.2 %all-gather.3.cloned.1.call-done = bf16[2048,4096]{1,0:T(8,128)(2,1)} async-done(((bf16[256,4096]{1,0:T(8,128)(2,1)}), bf16[2048,4096]{1,0:T(8,128)(2,1)}) %all-gather.3.cloned.1.call-update) | async-done | bytes 16777232 | tf_op jit(solution)/shard_map/all_gather | solution.py:37
  358.4 4.4 collective-permute-start.1
  362.7 126.8 %collective-permute-start = (bf16[2048,4096]{1,0:T(8,128)(2,1)}, bf16[2048,4096]{1,0:T(8,128)(2,1)}, u32[]{:S(2)}, u32[]{:S(2)}) collective-permute-start(bf16[2048,4096]{1,0:T(8,128)(2,1)} %all-gather.3.cloned.1.call-done), channel_id=1, source_target_pairs={{0,0},{1,1},{10,2},{11,3},{20,4},{21,5},{30,6},{31,7},{8,8},{9,9},... | collective-permute-start | bytes 50331656 | tf_op jit(solution)/shard_map/ppermute | solution.py:42
  489.6 0.0 collective-permute-done.2
  489.6 231.8 %collective-permute-done.1 = bf16[2048,4096]{1,0:T(8,128)(2,1)} collective-permute-done((bf16[2048,4096]{1,0:T(8,128)(2,1)}, bf16[2048,4096]{1,0:T(8,128)(2,1)}, u32[]{:S(2)}, u32[]{:S(2)}) %collective-permute-start.1) | collective-permute-done | bytes 16777248 | tf_op jit(solution)/shard_map/ppermute | solution.py:46
  721.3 0.0 collective-permute-done
  721.3 45.0 %fusion.1 = f32[2048,4096]{1,0:T(8,128)} fusion(bf16[2048,4096]{1,0:T(8,128)(2,1)} %collective-permute-done.2, s32[]{:T(128)S(6)} %select_n.16, bf16[2048,4096]{1,0:T(8,128)(2,1)} %collective-permute-done, bf16[2048,4096]{1,0:T(8,128)(2,1)} %collective-permute-done.1), kind=kOutput, calls=%fused_computation.3 | convolution fusion | flops 34376515584 | bytes 83886080 | tf_op jit(solution)/shard_map/dot_general | solution.py:51
  766.4 0.0 reduce-scatter.2.cloned.1.call-update
  766.4 691.4 %reduce-scatter.2.cloned.1.call-done = f32[256,4096]{1,0:T(8,128)} async-done(((f32[2048,4096]{1,0:T(8,128)}), f32[256,4096]{1,0:T(8,128)}) %reduce-scatter.2.cloned.1.call-update) | async-done | bytes 4194320 | tf_op jit(solution)/shard_map/reduce_scatter | solution.py:59
  1457.8 3.8 convert_element_type.3
Async XLA Ops:
  6.5 178.8 %all-gather.5.cloned.1.call-start = ((), (), s32[]{:S(2)}) async-start(), calls=%async_computation.2 | async-start | bytes 18874368 | tf_op jit(solution)/shard_map/all_gather | solution.py:38
  7.3 351.1 %all-gather.3.cloned.1.call-start = ((), (), s32[]{:S(2)}) async-start(), calls=%async_computation.1 | async-start | bytes 18874368 | tf_op jit(solution)/shard_map/all_gather | solution.py:37
  8.0 1449.8 %reduce-scatter.2.cloned.1.call-start = ((), (), s32[]{:S(2)}) async-start(), calls=%async_computation.3 | async-start | bytes 37748736 | tf_op jit(solution)/shard_map/reduce_scatter | solution.py:59
  185.3 304.2 %collective-permute-start.2 = (bf16[2048,4096]{1,0:T(8,128)(2,1)}, bf16[2048,4096]{1,0:T(8,128)(2,1)}, u32[]{:S(2)}, u32[]{:S(2)}) collective-permute-start(bf16[2048,4096]{1,0:T(8,128)(2,1)} %all-gather.5.cloned.1.call-done), channel_id=1, source_target_pairs={{0,0},{1,1},{2,2},{3,3},{4,4},{5,5},{6,6},{7,7},{10,8},{11,9},{12,... | collective-permute-start | bytes 50331656 | tf_op jit(solution)/shard_map/ppermute | solution.py:41
  358.4 363.0 %collective-permute-start.1 = (bf16[2048,4096]{1,0:T(8,128)(2,1)}, bf16[2048,4096]{1,0:T(8,128)(2,1)}, u32[]{:S(2)}, u32[]{:S(2)}) collective-permute-start(bf16[2048,4096]{1,0:T(8,128)(2,1)} %all-gather.3.cloned.1.call-done), channel_id=1, source_target_pairs={{8,0},{9,1},{18,2},{19,3},{28,4},{29,5},{6,6},{7,7},{16,8},{17,9},... | collective-permute-start | bytes 50331656 | tf_op jit(solution)/shard_map/ppermute | solution.py:46
  362.7 358.6 %collective-permute-start = (bf16[2048,4096]{1,0:T(8,128)(2,1)}, bf16[2048,4096]{1,0:T(8,128)(2,1)}, u32[]{:S(2)}, u32[]{:S(2)}) collective-permute-start(bf16[2048,4096]{1,0:T(8,128)(2,1)} %all-gather.3.cloned.1.call-done), channel_id=1, source_target_pairs={{0,0},{1,1},{10,2},{11,3},{20,4},{21,5},{30,6},{31,7},{8,8},{9,9},... | collective-permute-start | bytes 50331656 | tf_op jit(solution)/shard_map/ppermute | solution.py:42
Sparse Core Ops, SparseCore 0:
  9.1 176.1 all-gather.4
  187.1 171.2 all-gather.2
  766.5 691.2 reduce-scatter.1
where the time goes:
time: 1490 us; the launch traced here: 1470 us
  waiting for transfers between devices  1150 us (77%)
  starting transfers between devices  258 us (17%)
  matrix products  45 us (3%)
    reduce_scatter x1, waiting for transfers between devices, local_product(): lax.psum_scatter(part_sum, 'depth', scatter_dimension=0, tiled=True)  691 us
    ppermute x1, waiting for transfers between devices, local_product(): a_tail = lax.ppermute(a_full, all_axes, a_after)  232 us
    all_gather x1, waiting for transfers between devices, local_product(): b_full = lax.all_gather(b_blk, 'depth', axis=0, tiled=True)  177 us
    ppermute x1, starting transfers between devices, local_product(): a_lead = lax.ppermute(a_full, all_axes, a_start)  127 us
    ppermute x1, starting transfers between devices, local_product(): b_cur = lax.ppermute(b_full, all_axes, b_start)  127 us
    all_gather x1, waiting for transfers between devices, local_product(): a_full = lax.all_gather(a_blk, 'depth', axis=0, tiled=True)  46.2 us
    dot_general x1, matrix products, local_product(): part_sum = jnp.dot(pieces[0], b_cur, preferred_element_type=jnp.float32)  45 us
  transfers between devices with their start and end apart: 6, of which 4 were waited for; matrix products, arithmetic and copies ran while one was open for 0% of the time, Pallas kernels for 0%

commit v1 on v0

v1 whole, which is shorter than its diff:
```python
import jax
import jax.numpy as jnp
from jax import lax
from jax.sharding import PartitionSpec as P


def solution(mesh):
    def local_product(a_blk, b_blk):
        b_full = lax.all_gather(b_blk, "depth", axis=0, tiled=True)
        a_rows = lax.all_gather(a_blk, "col", axis=1, tiled=True)
        a_k = lax.all_to_all(a_rows, "row", split_axis=1, concat_axis=0, tiled=True)
        part = jnp.dot(a_k, b_full, preferred_element_type=jnp.float32)
        c_part = lax.psum_scatter(part, "row", scatter_dimension=0, tiled=True)
        return c_part.astype(jnp.bfloat16)

    block_spec = P(("row", "depth"), "col")
    return jax.shard_map(local_product, mesh=mesh, in_specs=(block_spec, block_spec), out_specs=block_spec, check_vma=False)
```

time: 1490 us -> 502 us (0.34); the launches traced: 1470 us -> 501 us
  waiting for transfers between devices: 1150 us -> 325 us
  starting transfers between devices: 258 us -> 0.08 us
  blocking collectives: 0 us -> 100 us
  local copies, waits for them, and re-layouts: 0 us -> 15.5 us
    reduce_scatter x1, waiting for transfers between devices: 691 us -> 172 us  [local_product(): c_part = lax.psum_scatter(part, 'row', scatter_dimension=0, tiled=True)]
    ppermute x3 -> x0, starting transfers between devices: 258 us -> none  [the longest x1 127 us: local_product(): a_lead = lax.ppermute(a_full, all_axes, a_start)]
    ppermute x3 -> x0, waiting for transfers between devices: 232 us -> none  [the longest x1 232 us: local_product(): a_tail = lax.ppermute(a_full, all_axes, a_after)]
    all_gather x1, waiting for transfers between devices: 177 us -> 64 us  [local_product(): b_full = lax.all_gather(b_blk, 'depth', axis=0, tiled=True)]
    all_to_all x0 -> x1, blocking collectives: none -> 100 us  [local_product(): a_k = lax.all_to_all(a_rows, 'row', split_axis=1, concat_axis=0, tiled=True)]
    all_gather x1, waiting for transfers between devices: 46.2 us -> 88.8 us  [local_product(): a_rows = lax.all_gather(a_blk, 'col', axis=1, tiled=True)]
  transfers between devices with their start and end apart: 6 -> 3, of which waited for: 4 -> 3; matrix products, arithmetic and copies ran while one was open for 0% -> 2% of each run, Pallas kernels for 0% -> 0%
where the time goes in v1:
time: 502 us; the launch traced here: 501 us
  waiting for transfers between devices  325 us (65%)
  blocking collectives  100 us (20%)
  matrix products  43.5 us (9%)
  local copies, waits for them, and re-layouts  15.5 us (3%)
  between operations  13.1 us (3%)
    reduce_scatter x1, waiting for transfers between devices, local_product(): c_part = lax.psum_scatter(part, 'row', scatter_dimension=0, tiled=True)  172 us
    all_to_all x1, blocking collectives, local_product(): a_k = lax.all_to_all(a_rows, 'row', split_axis=1, concat_axis=0, tiled=True)  100 us
    all_gather x1, waiting for transfers between devices, local_product(): a_rows = lax.all_gather(a_blk, 'col', axis=1, tiled=True)  88.8 us
    all_gather x1, waiting for transfers between devices, local_product(): b_full = lax.all_gather(b_blk, 'depth', axis=0, tiled=True)  64 us
    dot_general x1, matrix products, local_product(): part = jnp.dot(a_k, b_full, preferred_element_type=jnp.float32)  43.5 us
    all_to_all x1, local copies, waits for them, and re-layouts, local_product(): a_k = lax.all_to_all(a_rows, 'row', split_axis=1, concat_axis=0, tiled=True)  11.5 us
  transfers between devices with their start and end apart: 3, of which 3 were waited for; matrix products, arithmetic and copies ran while one was open for 2% of the time, Pallas kernels for 0%

profile of v1, /device:TPU:1, one launch (start us, length us, event | category | flops | bytes accessed | tf_op | source)
XLA Modules:
  0.0 501.0 jit_solution(1337435531689196432)
XLA Ops:
  6.5 0.0 all-gather.3.cloned.1.call-start
  6.5 4.1 copy.3
  10.6 0.0 all-gather.3.cloned.1.call-update
  10.6 0.0 all-gather.5.cloned.1.call-start
  10.7 0.7 all-gather.5.cloned.1.call-update
  11.4 0.0 reduce-scatter.2.cloned.1.call-start
  11.4 88.8 %all-gather.3.cloned.1.call-done = bf16[256,16384]{0,1:T(8,128)(2,1)} async-done(((bf16[256,4096]{0,1:T(8,128)(2,1)}), bf16[256,16384]{0,1:T(8,128)(2,1)}) %all-gather.3.cloned.1.call-update) | async-done | bytes 8388624 | tf_op jit(solution)/shard_map/all_gather | solution.py:10
  100.2 100.0 %all_to_all.19 = bf16[256,8,2048]{0,2,1:T(8,128)(2,1)} all-to-all(bf16[256,8,2048]{0,2,1:T(8,128)(2,1)} %bitcast.6), channel_id=1, replica_groups=mesh['depth'=8,'col'=4,'row'=8] {'row'}, dimensions={1} | all-to-all | bytes 16777216 | tf_op jit(solution)/shard_map/all_to_all | solution.py:11
  200.2 11.5 %copy.4 = bf16[8,256,2048]{2,1,0:T(8,128)(2,1)} copy(bf16[8,256,2048]{1,2,0:T(8,128)(2,1)} %bitcast.5) | data formatting | bytes 16777216 | tf_op jit(solution)/shard_map/all_to_all | solution.py:11
  211.6 64.0 %all-gather.5.cloned.1.call-done = bf16[2048,4096]{1,0:T(8,128)(2,1)} async-done(((bf16[256,4096]{1,0:T(8,128)(2,1)}), bf16[2048,4096]{1,0:T(8,128)(2,1)}) %all-gather.5.cloned.1.call-update) | async-done | bytes 16777232 | tf_op jit(solution)/shard_map/all_gather | solution.py:9
  275.6 43.5 %fusion = f32[2048,4096]{1,0:T(8,128)} fusion(bf16[2048,2048]{1,0:T(8,128)(2,1)} %bitcast.7, bf16[2048,4096]{1,0:T(8,128)(2,1)} %all-gather.5.cloned.1.call-done), kind=kOutput, calls=%fused_computation | convolution fusion | flops 34359738368 | bytes 58720256 | tf_op jit(solution)/shard_map/dot_general | solution.py:12
  319.1 0.0 reduce-scatter.2.cloned.1.call-update
  319.1 171.6 %reduce-scatter.2.cloned.1.call-done = f32[256,4096]{1,0:T(8,128)} async-done(((f32[2048,4096]{1,0:T(8,128)}), f32[256,4096]{1,0:T(8,128)}) %reduce-scatter.2.cloned.1.call-update) | async-done | bytes 4194320 | tf_op jit(solution)/shard_map/reduce_scatter | solution.py:13
  490.7 3.8 convert_element_type.3
Async XLA Ops:
  6.5 93.7 %all-gather.3.cloned.1.call-start = ((), (), s32[]{:S(2)}) async-start(), calls=%async_computation.2 | async-start | bytes 10485760 | tf_op jit(solution)/shard_map/all_gather | solution.py:10
  10.6 265.0 %all-gather.5.cloned.1.call-start = ((), (), s32[]{:S(2)}) async-start(), calls=%async_computation.3 | async-start | bytes 18874368 | tf_op jit(solution)/shard_map/all_gather | solution.py:9
  11.4 479.3 %reduce-scatter.2.cloned.1.call-start = ((), (), s32[]{:S(2)}) async-start(), calls=%async_computation.4 | async-start | bytes 37748736 | tf_op jit(solution)/shard_map/reduce_scatter | solution.py:13
Sparse Core Ops, SparseCore 0:
  10.7 89.4 all-gather.2
  102.0 173.5 all-gather.4
  319.3 171.4 reduce-scatter.1

commit v2 on v1

v2 whole, which is shorter than its diff:
```python
import functools

import jax
import jax.numpy as jnp
from jax import lax
from jax.experimental import pallas as pl
from jax.experimental.pallas import tpu as pltpu
from jax.sharding import PartitionSpec as P

MESH = pl.DeviceIdType.MESH
X_N, Y_N, Z_N = 4, 4, 8
CHUNKS = 16
C0_SLOTS = 4
OUT_SLOTS = 4

A_SCHEDULE = (
    (-1, ("s1", 0)), (0, ("r1", 0)), (3, ("s1", 1)), (4, ("s2", 0)), (4, ("s2f", 0)), (5, ("r1", 1)),
    (8, ("ag", 0)), (8, ("s2f", 1)), (8, ("s2", 1)), (8, ("r2", 0)), (11, ("r2", 1)), (11, ("fw", 0, 0)),
    (12, ("fw", 0, 1)), (14, ("ag", 1)), (15, ("gw", 0)), (18, ("fw", 1, 0)), (19, ("fw", 1, 1)),
    (22, ("ag", 2)), (22, ("gw", 1)), (25, ("fw", 2, 0)), (26, ("fw", 2, 1)), (29, ("ag", 3)), (29, ("gw", 2)),
    (38, ("fw", 3, 0)), (43, ("fw", 3, 1)), (45, ("gw", 3)),
)
C_BASE = (10, 14, 19, 28)
C_START = (15, 22, 29, 45)


def kernel(a_hbm, b_hbm, c_hbm, a_all, s1, rl1, rl2, b_all, crecv, c0, outst,
           bl_sem, zr_sem, zs_sem, dr_sem, s1_sem, r1_sem, r2_sem, s2_sem, ag_sem, fw_sem, as_sem,
           cr_sem, cs_sem, c0_sem, out_sem):
    row, y, z = lax.axis_index("row"), lax.axis_index("col"), lax.axis_index("depth")
    x, c = row // 2, row % 2
    width = b_all.shape[3]
    rows_q = s1.shape[2]
    half = rows_q // 2
    lo, hi = pl.ds(0, half), pl.ds(half, half)

    def at_x(dx):
        return {"row": 2 * ((x + dx + X_N) % X_N) + c}

    def at_y(dy):
        return {"col": (y + dy + Y_N) % Y_N}

    step = 1 - 2 * c
    z_long = {"depth": (z + step + Z_N) % Z_N}
    z_short = {"depth": (z - step + Z_N) % Z_N}
    partner = {"row": 2 * x + 1 - c}

    def send(src, dst, ssem, rsem, dev):
        pltpu.make_async_remote_copy(src_ref=src, dst_ref=dst, send_sem=ssem, recv_sem=rsem,
                                     device_id=dev, device_id_type=MESH).start()

    def wait(ref, sem):
        pltpu.make_async_copy(ref, ref, sem).wait()

    e_own = (y - x + Y_N) % Y_N
    flip = e_own // 3
    j_own = e_own

    def b_local(m):
        return pltpu.make_async_copy(b_hbm.at[:, pl.ds(pl.multiple_of(m * width, width), width)],
                                     b_all.at[m, c * Z_N + z], bl_sem.at[m])

    b_local(0).start()

    barrier = pltpu.get_barrier_semaphore()
    for dev in (at_x(1), at_x(-1), at_y(1), at_y(-1), z_long, z_short, partner):
        pl.semaphore_signal(barrier, inc=1, device_id=dev, device_id_type=MESH)
    lax.fori_loop(1, CHUNKS, lambda m, _: (b_local(m).start(), 0)[1], 0)
    pl.semaphore_wait(barrier, 7)

    def s1_dst(e, o, j, rows=None):
        def final():
            return a_all.at[3, o, j] if rows is None else a_all.at[3, o, j, rows]

        def staged():
            return s1.at[(e + Y_N - 1) % Y_N, o] if rows is None else s1.at[(e + Y_N - 1) % Y_N, o, rows]
        return final, staged

    def by_e(e, o, j, rows, fn):
        final, staged = s1_dst(e, o, j, rows)

        @pl.when(e == 0)
        def _():
            fn(final())

        @pl.when(e != 0)
        def _():
            fn(staged())

    def a_event(event):
        kind = event[0]
        if kind == "s1":
            o = event[1]
            h = (o + flip) % 2
            send(a_hbm.at[h, 2, lo], rl1.at[0, o], as_sem.at[0], r1_sem.at[0, o], at_y(1))
            send(a_hbm.at[h, 2, hi], rl1.at[1, o], as_sem.at[0], r1_sem.at[1, o], at_y(-1))
            sem = s1_sem.at[e_own, o]
            by_e(e_own, o, 1, None, lambda dst: send(a_hbm.at[h, 1], dst, as_sem.at[0], sem, at_y(1)))
            by_e(e_own, o, 3, None, lambda dst: send(a_hbm.at[h, 3], dst, as_sem.at[0], sem, at_y(-1)))
            by_e(e_own, o, 0, None, lambda dst: pltpu.make_async_copy(a_hbm.at[h, 0], dst, sem).start())
        elif kind == "r1":
            o = event[1]
            for d, dy, rows in ((0, 1, lo), (1, -1, hi)):
                e = (y - dy - x + 2 * Y_N) % Y_N
                wait(rl1.at[d, o], r1_sem.at[d, o])
                by_e(e, o, 2, rows, lambda dst: send(rl1.at[d, o], dst, as_sem.at[0], s1_sem.at[e, o], at_y(dy)))
        elif kind == "s2":
            o = event[1]
            wait(s1.at[0, o], s1_sem.at[1, o])
            wait(s1.at[2, o], s1_sem.at[3, o])
            g = 2 * o
            j = (y - x - 1 + 2 * Y_N) % Y_N
            send(s1.at[0, o], a_all.at[g, o, j], as_sem.at[1], s2_sem.at[g, o], at_x(1))
            j = (y - x + 1 + Y_N) % Y_N
            send(s1.at[2, o], a_all.at[g, 1 - o, j], as_sem.at[1], s2_sem.at[g, 1 - o], at_x(-1))
        elif kind == "s2f":
            o = event[1]
            wait(s1.at[1, o], s1_sem.at[2, o])
            send(s1.at[1, o, lo], rl2.at[0, o], as_sem.at[1], r2_sem.at[0, o], at_x(1))
            send(s1.at[1, o, hi], rl2.at[1, o], as_sem.at[1], r2_sem.at[1, o], at_x(-1))
        elif kind == "r2":
            o = event[1]
            for d, dx, rows in ((0, 1, lo), (1, -1, hi)):
                j = (y - x - dx + 2 * Y_N) % Y_N
                wait(rl2.at[d, o], r2_sem.at[d, o])
                send(rl2.at[d, o], a_all.at[1, o, j, rows], as_sem.at[1], s2_sem.at[1, o], at_x(dx))
        elif kind == "ag":
            g = event[1]
            for d in range(2):
                mine = a_all.at[g, d, j_own]
                wait(mine, s1_sem.at[0, d] if g == 3 else s2_sem.at[g, d])
                send(mine, mine, as_sem.at[2 + g], ag_sem.at[g, d, 0], at_y(1))
                send(mine, mine, as_sem.at[2 + g], ag_sem.at[g, d, 1], at_y(-1))
        elif kind == "fw":
            g, d = event[1:]
            for k, dy, rows in ((0, 1, lo), (1, -1, hi)):
                j = (y - dy - x + 2 * Y_N) % Y_N
                wait(a_all.at[g, d, j], ag_sem.at[g, d, k])
                part = a_all.at[g, d, j, rows]
                send(part, part, as_sem.at[2 + g], fw_sem.at[g, d, k], at_y(dy))
        elif kind == "gw":
            g = event[1]
            for d in range(2):
                j = (j_own + 2) % Y_N
                wait(a_all.at[g, d, j, lo], fw_sem.at[g, d, 0])
                wait(a_all.at[g, d, j, hi], fw_sem.at[g, d, 1])

    def block(hop):
        return c * Z_N + (z - hop * step + 2 * Z_N) % Z_N

    def hand_over(m, kb):
        send(b_all.at[m, kb], b_all.at[m, kb], zs_sem.at[m], dr_sem.at[m], partner)

    def forward_long(m, hop):
        piece = b_all.at[m, block(hop)]
        send(piece, piece, zs_sem.at[m], zr_sem.at[m, hop], z_long)

    def forward_short(m, hop):
        piece = b_all.at[m, block(-hop)]
        send(piece, piece, zs_sem.at[m], zr_sem.at[m, 4 + hop], z_short)

    def b_own(m):
        b_local(m).wait()
        forward_long(m, 0)
        forward_short(m, 0)
        hand_over(m, block(0))

    def b_hop(m, hop):
        wait(b_all.at[m, block(hop)], zr_sem.at[m, hop - 1])
        forward_long(m, hop)
        hand_over(m, block(hop))
        wait(b_all.at[m, block(-hop)], zr_sem.at[m, 4 + hop - 1])
        if hop < 3:
            forward_short(m, hop)
        hand_over(m, block(-hop))

    def b_last(m):
        wait(b_all.at[m, block(4)], zr_sem.at[m, 3])
        hand_over(m, block(4))

    def in_range(m):
        return (m >= 0) & (m < CHUNKS)

    def b_slot(s):
        t, u = s // 4, s % 4
        pl.when((u == 0) & in_range(t + 1))(lambda: b_own(t + 1))
        pl.when((u == 1) & in_range(t - 1))(lambda: b_hop(t - 1, 2))
        pl.when((u == 1) & in_range(t - 2))(lambda: b_last(t - 2))
        pl.when((u == 2) & in_range(t))(lambda: b_hop(t, 1))
        pl.when((u == 3) & in_range(t - 1))(lambda: b_hop(t - 1, 3))

    def product(g, m):
        a = a_all[g].reshape(-1, a_all.shape[-1])
        b = b_all[m].reshape(-1, width)
        return jnp.dot(a, b, preferred_element_type=jnp.float32).reshape(crecv.shape[2:])

    def c_stage(g, m):
        if g == 0:
            eight = b_all.at[m, pl.ds(0, Z_N)]
            wait(eight, dr_sem.at[m])
            slot = m % C0_SLOTS

            @pl.when(m >= C0_SLOTS)
            def _():
                wait(c0.at[slot], c0_sem.at[slot])
            c0[slot] = product(0, m)
            src, ssem = c0.at[slot], c0_sem.at[slot]
        else:
            part = product(g, m)
            for d in range(2):
                wait(crecv.at[m, g - 1, d], cr_sem.at[m, g - 1, d])
            if g == 3:
                slot = m % OUT_SLOTS

                @pl.when(m >= OUT_SLOTS)
                def _():
                    out_copy(m - OUT_SLOTS).wait()
                outst[slot] = (crecv[m, g - 1] + part).reshape(outst.shape[1:]).astype(outst.dtype)
                out_copy(m).start()
                return
            crecv[m, g - 1] += part
            src, ssem = crecv.at[m, g - 1], cs_sem.at[m]
        send(src.at[0], crecv.at[m, g, 0], ssem, cr_sem.at[m, g, 0], at_x(1))
        send(src.at[1], crecv.at[m, g, 1], ssem, cr_sem.at[m, g, 1], at_x(-1))

    def out_copy(m):
        return pltpu.make_async_copy(outst.at[m % OUT_SLOTS],
                                     c_hbm.at[:, pl.ds(pl.multiple_of(m * width, width), width)],
                                     out_sem.at[m % OUT_SLOTS])

    def c_slot(s):
        for g in (3, 2, 1, 0):
            base, start = C_BASE[g], C_START[g]
            cross = max(start - base, 0)
            m_late = (s - base) // 4
            late = ((s - base) % 4 == 0) & (m_late >= cross) & (m_late < CHUNKS)
            m_early = (s - start) // 3
            early = ((s - start) % 3 == 0) & (m_early >= 0) & (m_early < min(cross, CHUNKS))
            m = jnp.where(early, m_early, m_late)
            pl.when(early | late)(functools.partial(c_stage, g, m))

    for slot, event in A_SCHEDULE:
        if slot < 0:
            a_event(event)
    b_own(0)
    last_a = max(slot for slot, _ in A_SCHEDULE)
    n_slots = max(max(C_BASE[g] + 4 * (CHUNKS - 1), C_START[g] + 3 * (CHUNKS - 1)) for g in range(4)) + 1

    def first_part(s, carry):
        b_slot(s)
        for slot in sorted({slot for slot, _ in A_SCHEDULE if slot >= 0}):
            @pl.when(s == slot)
            def _():
                for at, event in A_SCHEDULE:
                    if at == slot:
                        a_event(event)
        c_slot(s)
        return carry

    def second_part(s, carry):
        b_slot(s)
        c_slot(s)
        return carry

    lax.fori_loop(0, last_a + 1, first_part, 0)
    lax.fori_loop(last_a + 1, n_slots, second_part, 0)

    def drain(m, carry):
        wait(b_all.at[m, pl.ds(0, 15)], zs_sem.at[m])
        wait(crecv.at[m, pl.ds(0, 2)], cs_sem.at[m])
        return carry

    lax.fori_loop(0, CHUNKS, drain, 0)
    wait(a_all.at[0], as_sem.at[0])
    wait(a_all.at[0], as_sem.at[1])
    for g in range(4):
        wait(a_all.at[0, :, pl.ds(0, 3)], as_sem.at[2 + g])
    for slot in range(C0_SLOTS):
        wait(c0.at[slot], c0_sem.at[slot])
    for m in range(CHUNKS - OUT_SLOTS, CHUNKS):
        out_copy(m).wait()


def solution(mesh):
    def local_product(a_blk, b_blk):
        rows, cols = a_blk.shape
        width = cols // CHUNKS
        rows_q = rows // 8
        dma = pltpu.SemaphoreType.DMA
        return pl.pallas_call(
            kernel,
            name="matmul_3d",
            out_shape=jax.ShapeDtypeStruct((rows, cols), jnp.bfloat16),
            in_specs=[pl.BlockSpec(memory_space=pl.ANY)] * 2,
            out_specs=pl.BlockSpec(memory_space=pl.ANY),
            scratch_shapes=[
                pltpu.VMEM((4, 2, 4, rows_q, cols), jnp.bfloat16),
                pltpu.VMEM((3, 2, rows_q, cols), jnp.bfloat16),
                pltpu.VMEM((2, 2, rows_q // 2, cols), jnp.bfloat16),
                pltpu.VMEM((2, 2, rows_q // 2, cols), jnp.bfloat16),
                pltpu.VMEM((CHUNKS, 2 * Z_N, rows, width), jnp.bfloat16),
                pltpu.VMEM((CHUNKS, 3, 2, rows // 2, width), jnp.float32),
                pltpu.VMEM((C0_SLOTS, 2, rows // 2, width), jnp.float32),
                pltpu.VMEM((OUT_SLOTS, rows, width), jnp.bfloat16),
                dma((CHUNKS,)), dma((CHUNKS, 7)), dma((CHUNKS,)), dma((CHUNKS,)),
                dma((4, 2)), dma((2, 2)), dma((2, 2)), dma((3, 2)), dma((4, 2, 2)), dma((4, 2, 2)), dma((6,)),
                dma((CHUNKS, 3, 2)), dma((CHUNKS,)), dma((C0_SLOTS,)), dma((OUT_SLOTS,)),
            ],
            compiler_params=pltpu.CompilerParams(
                collective_id=0, has_side_effects=True, vmem_limit_bytes=67043328
            ),
        )(a_blk.reshape(2, 4, rows_q, cols), b_blk)

    block_spec = P(("row", "depth"), "col")
    return jax.shard_map(local_product, mesh=mesh, in_specs=(block_spec, block_spec), out_specs=block_spec, check_vma=False)
```

time: 502 us -> 209 us (0.42)
  waiting for transfers between devices: 325 us -> 0 us
  Pallas kernels: 0 us -> 204 us
  blocking collectives: 100 us -> 0 us
  matrix products: 43.5 us -> 0 us
  between operations: 13.1 us -> 0.01 us
  local copies, waits for them, and re-layouts: 15.5 us -> 3.13 us
    pallas_call x0 -> x1, Pallas kernels: none -> 204 us  [local_product(): pl.pallas_call(kernel, name='matmul_3d', out_shape=jax.ShapeDtypeStruct((...]
    reduce_scatter x1 -> x0, waiting for transfers between devices: 172 us -> none  [local_product(): c_part = lax.psum_scatter(part, 'row', scatter_dimension=0, tiled=True)]
    all_gather x2 -> x0, waiting for transfers between devices: 153 us -> none  [the longest x1 88.8 us: local_product(): a_rows = lax.all_gather(a_blk, 'col', axis=1, tiled=True)]
    all_to_all x1 -> x0, blocking collectives: 100 us -> none  [local_product(): a_k = lax.all_to_all(a_rows, 'row', split_axis=1, concat_axis=0, tiled=True)]
    dot_general x1 -> x0, matrix products: 43.5 us -> none  [local_product(): part = jnp.dot(a_k, b_full, preferred_element_type=jnp.float32)]
    all_to_all x1 -> x0, local copies, waits for them, and re-layouts: 11.5 us -> none  [local_product(): a_k = lax.all_to_all(a_rows, 'row', split_axis=1, concat_axis=0, tiled=True)]
  transfers between devices with their start and end apart: 3 -> 0, of which waited for: 3 -> 0; matrix products, arithmetic and copies ran while one was open for 2% -> 0% of each run, Pallas kernels for 0% -> 0%
where the time goes in v2:
time: 209 us; the launch traced here: 207 us
  Pallas kernels  204 us (98%)
  local copies, waits for them, and re-layouts  3.13 us (1%)
    pallas_call x1, Pallas kernels, local_product(): pl.pallas_call(kernel, name='matmul_3d', out_shape=jax.ShapeDtypeStruct((...  204 us

profile of v2, /device:TPU:1, one launch (start us, length us, event | category | flops | bytes accessed | tf_op | source)
XLA Modules:
  0.0 206.9 jit_solution(11578625014076803474)
XLA Ops:
  0.0 203.8 %matmul_3d.1 = bf16[256,4096]{1,0:T(8,128)(2,1)} custom-call(bf16[2,4,32,4096]{3,2,1,0:T(8,128)(2,1)} %bitcast.1, bf16[256,4096]{1,0:T(8,128)(2,1)} %b_hbm.1), custom_call_target="tpu_custom_call" | custom-call | tf_op jit(solution)/shard_map/matmul_3d/pallas_call | solution.py:290
  203.8 3.1 %copy.4 = bf16[256,4096]{1,0:T(8,128)(2,1)} copy(bf16[256,4096]{1,0:T(8,128)(2,1)} %matmul_3d.1) | data formatting | bytes 4194304

commit v3 on v1

v3 whole, which is shorter than its diff:
```python
import jax
import jax.numpy as jnp
from jax import lax
from jax.experimental import pallas as pl
from jax.experimental.pallas import tpu as pltpu
from jax.sharding import PartitionSpec as P

MESH = pl.DeviceIdType.MESH
X_N, Y_N, Z_N = 4, 4, 8
BLOCKS = 16
SLOTS = 4
LOOP = 8
S1, R1, S2, S2F, R2, AG, FW, OWN, LONG, SHORT, SUM = range(11)
WIDE = 14
SPLIT = 4
ALL = 2
ORDER = (
    (7, 0), (0, 0, 0), (7, 1), (0, 0, 1), (7, 2), (1, 0, 0, 1), (1, 0, 0, 0), (0, 1, 0), (7, 3), (1, 0, 1, 1),
    (9, 1, 1), (8, 1, 1), (2, 0, 0), (1, 0, 1, 0), (0, 1, 1), (8, 0, 1), (9, 3, 1), (8, 2, 1), (9, 2, 1), (2, 0, 1),
    (9, 1, 2), (1, 1, 0, 0), (1, 1, 0, 1), (9, 0, 1), (5, 0, 0, 1), (8, 0, 2), (5, 0, 0, 0), (1, 1, 1, 1),
    (1, 1, 1, 0), (8, 1, 2), (3, 1, 0), (2, 1, 0), (9, 3, 2), (8, 3, 1), (5, 0, 1, 1), (3, 0, 0), (8, 2, 2),
    (6, 0, 0, 1), (5, 0, 1, 0), (4, 1, 0, 0), (7, 4), (4, 1, 0, 1), (3, 1, 1), (8, 3, 2), (8, 2, 3), (9, 1, 3),
    (9, 2, 2), (5, 1, 0, 1), (8, 0, 3), (3, 0, 1), (6, 0, 1, 1), (4, 0, 0, 1), (9, 0, 2), (8, 1, 3), (8, 4, 1),
    (4, 1, 1, 1), (8, 3, 3), (4, 0, 0, 0), (6, 0, 0, 0), (4, 0, 1, 0), (4, 1, 1, 0), (2, 1, 1), (6, 0, 1, 0),
    (4, 0, 1, 1), (5, 1, 0, 0), (7, 5), (6, 1, 0, 1), (8, 0, 4), (8, 2, 4), (9, 3, 3), (9, 0, 3), (9, 2, 3),
    (10, 0, 0, 0), (8, 1, 4), (5, 1, 1, 1), (9, 4, 1), (10, 2, 0, 0), (8, 4, 2), (10, 2, 0, 1), (10, 1, 0, 0),
    (6, 1, 0, 0), (5, 1, 1, 0), (7, 6), (8, 3, 4), (10, 3, 0, 1), (5, 2, 0, 0), (10, 3, 0, 0), (9, 4, 2),
    (10, 0, 0, 1), (8, 5, 1), (8, 4, 3), (10, 2, 1, 0), (8, 6, 1), (5, 2, 0, 1), (10, 0, 1, 0), (9, 5, 1),
    (10, 1, 0, 1), (10, 1, 1, 0), (6, 1, 1, 1), (6, 1, 1, 0), (9, 6, 1), (8, 5, 2), (10, 3, 1, 0), (8, 4, 4),
    (5, 2, 1, 0), (6, 2, 0, 0), (7, 7), (9, 4, 3), (10, 4, 0, 2), (9, 5, 2), (8, 6, 2), (10, 3, 1, 1), (5, 2, 1, 1),
    (10, 1, 1, 1), (8, 5, 3), (9, 6, 2), (10, 2, 1, 1), (7, 8), (6, 2, 0, 1), (6, 2, 1, 0), (10, 0, 1, 1),
    (10, 4, 1, 2), (9, 5, 3), (8, 7, 1), (8, 6, 3), (6, 2, 1, 1), (5, 3, 1, 0), (8, 5, 4), (10, 2, 2, 0),
    (10, 5, 0, 2), (7, 9), (10, 3, 2, 1), (10, 4, 2, 2), (9, 6, 3), (9, 7, 1), (8, 8, 1), (5, 3, 0, 0), (8, 7, 2),
    (5, 3, 1, 1), (10, 2, 2, 1), (8, 6, 4), (8, 9, 1), (10, 6, 0, 2), (7, 10), (10, 0, 2, 1), (8, 8, 2),
    (10, 5, 1, 2), (6, 3, 0, 0), (10, 1, 2, 1), (8, 7, 3), (5, 3, 0, 1), (9, 8, 1), (8, 9, 2), (10, 6, 1, 2),
    (9, 7, 2), (6, 3, 1, 1), (6, 3, 0, 1), (8, 8, 3), (7, 11), (10, 1, 2, 0), (10, 5, 2, 2), (6, 3, 1, 0), (9, 9, 1),
    (10, 0, 2, 0), (8, 7, 4), (8, 9, 3), (10, 3, 2, 0), (9, 7, 3), (9, 8, 2), (9, 10, 1), (10, 7, 0, 2), (8, 10, 1),
    (9, 9, 2), (10, 6, 2, 2), (8, 8, 4), (8, 11, 1), (9, 8, 3), (10, 8, 0, 2), (9, 11, 1), (10, 7, 1, 2), (8, 10, 2),
    (10, 0, 3, 0), (9, 10, 2), (8, 9, 4), (7, 12), (9, 9, 3), (10, 9, 0, 2), (10, 0, 3, 1), (8, 11, 2), (10, 8, 1, 2),
    (8, 10, 3), (8, 12, 1), (10, 7, 2, 2), (9, 12, 1), (8, 11, 3), (9, 10, 3), (9, 11, 2), (10, 9, 1, 2), (8, 10, 4),
    (7, 13), (10, 1, 3, 0), (10, 8, 2, 2), (8, 12, 2), (9, 12, 2), (7, 14), (10, 10, 0, 2), (10, 1, 3, 1),
    (10, 9, 2, 2), (8, 11, 4), (9, 11, 3), (8, 12, 3), (10, 11, 0, 2), (8, 13, 1), (10, 2, 3, 0), (10, 2, 3, 1),
    (9, 12, 3), (7, 15), (9, 14, 1), (10, 10, 1, 2), (9, 13, 1), (8, 12, 4), (7, 16), (10, 12, 0, 2), (10, 3, 3, 0),
    (8, 13, 2), (10, 11, 1, 2), (8, 16, 1), (8, 14, 1), (7, 17), (10, 3, 3, 1), (9, 13, 2), (8, 15, 1),
    (10, 10, 2, 2), (10, 4, 3, 2), (10, 12, 1, 2), (8, 13, 3), (8, 14, 2), (10, 11, 2, 2), (8, 16, 2), (9, 15, 1),
    (9, 14, 2), (9, 13, 3), (8, 13, 4), (8, 17, 1), (8, 15, 2), (9, 16, 1), (8, 14, 3), (10, 13, 0, 2),
    (10, 12, 2, 2), (8, 16, 3), (8, 17, 2), (8, 15, 3), (9, 15, 2), (9, 17, 1), (9, 16, 2), (9, 14, 3), (8, 14, 4),
    (10, 14, 0, 2), (8, 17, 3), (10, 13, 1, 2), (10, 5, 3, 2), (8, 15, 4), (9, 15, 3), (8, 16, 4), (9, 17, 2),
    (9, 16, 3), (10, 15, 0, 2), (10, 16, 0, 2), (10, 14, 1, 2), (9, 17, 3), (8, 17, 4), (10, 17, 0, 2),
    (10, 15, 1, 2), (10, 6, 3, 2), (10, 16, 1, 2), (10, 13, 2, 2), (10, 17, 1, 2), (10, 7, 3, 2), (10, 14, 2, 2),
    (10, 8, 3, 2), (10, 9, 3, 2), (10, 15, 2, 2), (10, 10, 3, 2), (10, 16, 2, 2), (10, 17, 2, 2), (10, 11, 3, 2),
    (10, 12, 3, 2), (10, 13, 3, 2), (10, 14, 3, 2), (10, 15, 3, 2), (10, 16, 3, 2), (10, 17, 3, 2),
)


def chunk(n):
    return (n, None) if n < WIDE else (WIDE + (n - WIDE) // 2, (n - WIDE) % 2)


CHUNKS = WIDE + 2 * (BLOCKS - WIDE)


def kernel(a_hbm, b_hbm, c_hbm, a_own, a_all, s1, rl1, rl2, b_all, crecv, c0, outst, prod,
           ld_sem, zr_sem, zs_sem, dr_sem, s1_sem, r1_sem, r2_sem, s2_sem, ag_sem, fw_sem, as_sem,
           cr_sem, cs_sem, c0_sem, out_sem):
    row, y, z = lax.axis_index("row"), lax.axis_index("col"), lax.axis_index("depth")
    x, c = row // 2, row % 2
    width = b_all.shape[3]
    narrow = width // 2
    cols = a_own.shape[4]
    part_cols = (pl.ds(0, cols // 2), pl.ds(cols // 2, cols // 2))
    rest = slice(None)

    def at_x(dx):
        return {"row": 2 * ((x + dx + X_N) % X_N) + c}

    def at_y(dy):
        return {"col": (y + dy + Y_N) % Y_N}

    step = 1 - 2 * c
    z_long = {"depth": (z + step + Z_N) % Z_N}
    z_short = {"depth": (z - step + Z_N) % Z_N}
    partner = {"row": 2 * x + 1 - c}

    def send(src, dst, ssem, rsem, dev):
        pltpu.make_async_remote_copy(src_ref=src, dst_ref=dst, send_sem=ssem, recv_sem=rsem,
                                     device_id=dev, device_id_type=MESH).start()

    def wait(ref, sem):
        pltpu.make_async_copy(ref, ref, sem).wait()

    e_own = (y - x + Y_N) % Y_N
    flip = e_own // 3
    j_own = e_own

    def b_local(m, sem):
        return pltpu.make_async_copy(b_hbm.at[:, pl.ds(pl.multiple_of(m * width, width), width)],
                                     b_all.at[m, c * Z_N + z], ld_sem.at[sem])

    a_load = pltpu.make_async_copy(a_hbm, a_own, ld_sem.at[2])
    a_load.start()
    b_local(0, 0).start()
    barrier = pltpu.get_barrier_semaphore()
    for dev in (at_x(1), at_x(-1), at_y(1), at_y(-1), z_long, z_short, partner):
        pl.semaphore_signal(barrier, inc=1, device_id=dev, device_id_type=MESH)
    lax.fori_loop(1, BLOCKS, lambda m, _: (b_local(m, 1).start(), 0)[1], 0)

    def by_e(e, o, r, j, part, fn):
        col_part = rest if part is None else part_cols[part]

        @pl.when(e == 0)
        def _():
            fn(a_all.at[3, o, j, r, :, col_part])

        @pl.when(e != 0)
        def _():
            fn(s1.at[(e + Y_N - 1) % Y_N, o, r, :, col_part])

    for o in range(2):
        for r in range(2):
            by_e(e_own, o, r, 0, None, lambda dst: pltpu.make_async_copy(
                a_hbm.at[(o + flip) % 2, 0, r], dst, s1_sem.at[e_own, o, r]).start())
    pl.semaphore_wait(barrier, 7)
    a_load.wait()

    def ev_s1(o, r):
        h = (o + flip) % 2
        send(a_own.at[h, 2, r, :, part_cols[0]], rl1.at[0, o, r], as_sem, r1_sem.at[0, o, r], at_y(1))
        send(a_own.at[h, 2, r, :, part_cols[1]], rl1.at[1, o, r], as_sem, r1_sem.at[1, o, r], at_y(-1))
        sem = s1_sem.at[e_own, o, r]
        by_e(e_own, o, r, 1, None, lambda dst: send(a_own.at[h, 1, r], dst, as_sem, sem, at_y(1)))
        by_e(e_own, o, r, 3, None, lambda dst: send(a_own.at[h, 3, r], dst, as_sem, sem, at_y(-1)))

    def ev_r1(o, r, d):
        dy = 1 - 2 * d
        e = (y - dy - x + 2 * Y_N) % Y_N
        wait(rl1.at[d, o, r], r1_sem.at[d, o, r])
        by_e(e, o, r, 2, d, lambda dst: send(rl1.at[d, o, r], dst, as_sem, s1_sem.at[e, o, r], at_y(dy)))

    def ev_s2(o, r):
        wait(s1.at[0, o, r], s1_sem.at[1, o, r])
        wait(s1.at[2, o, r], s1_sem.at[3, o, r])
        g = 2 * o
        j = (y - x - 1 + 2 * Y_N) % Y_N
        send(s1.at[0, o, r], a_all.at[g, o, j, r], as_sem, s2_sem.at[g, o, r], at_x(1))
        j = (y - x + 1 + Y_N) % Y_N
        send(s1.at[2, o, r], a_all.at[g, 1 - o, j, r], as_sem, s2_sem.at[g, 1 - o, r], at_x(-1))

    def ev_s2f(o, r):
        wait(s1.at[1, o, r], s1_sem.at[2, o, r])
        for d in range(2):
            send(s1.at[1, o, r, :, part_cols[d]], rl2.at[d, o, r], as_sem, r2_sem.at[d, o, r], at_x(1 - 2 * d))

    def ev_r2(o, r, d):
        dx = 1 - 2 * d
        j = (y - x - dx + 2 * Y_N) % Y_N
        wait(rl2.at[d, o, r], r2_sem.at[d, o, r])
        send(rl2.at[d, o, r], a_all.at[1, o, j, r, :, part_cols[d]], as_sem, s2_sem.at[1, o, r], at_x(dx))

    def ev_ag(g, r, d):
        quarter = a_all.at[g, d, j_own, r]
        wait(quarter, s1_sem.at[0, d, r] if g == 3 else s2_sem.at[g, d, r])
        send(quarter, quarter, as_sem, ag_sem.at[g, d, r], at_y(1))
        send(quarter, quarter, as_sem, ag_sem.at[g, d, r], at_y(-1))

    def ev_fw(g, r, d):
        wait(a_all.at[0, 0, 0], ag_sem.at[g, d, r])
        for k, dy in ((0, 1), (1, -1)):
            j = (y - dy - x + 2 * Y_N) % Y_N
            part = a_all.at[g, d, j, r, :, part_cols[k]]
            send(part, part, as_sem, fw_sem.at[g, r], at_y(dy))

    def group_complete(g, r):
        wait(a_all.at[0, 0, 0], fw_sem.at[g, r])

    def block(hop):
        return c * Z_N + (z - hop * step + 2 * Z_N) % Z_N

    def lanes_of(n):
        half = chunk(n)[1]
        return rest if half is None else pl.ds(half * narrow, narrow)

    def piece(n, kb):
        return b_all.at[chunk(n)[0], kb, :, lanes_of(n)]

    def hand_over(n, kb):
        send(piece(n, kb), piece(n, kb), zs_sem.at[chunk(n)[0] // 4], dr_sem.at[n], partner)

    def forward_long(n, hop):
        p = piece(n, block(hop))
        send(p, p, zs_sem.at[chunk(n)[0] // 4], zr_sem.at[n, hop], z_long)

    def forward_short(n, hop):
        p = piece(n, block(-hop))
        send(p, p, zs_sem.at[chunk(n)[0] // 4], zr_sem.at[n, 4 + hop], z_short)

    def ev_own(n):
        if n == 0:
            b_local(0, 0).wait()
        elif n == 1:
            wait(b_all.at[0, pl.ds(0, BLOCKS - 1)], ld_sem.at[1])
        forward_long(n, 0)
        forward_short(n, 0)
        hand_over(n, block(0))

    def ev_long(n, hop):
        wait(piece(n, block(hop)), zr_sem.at[n, hop - 1])
        if hop < 4:
            forward_long(n, hop)
        hand_over(n, block(hop))

    def ev_short(n, hop):
        wait(piece(n, block(-hop)), zr_sem.at[n, 4 + hop - 1])
        if hop < 3:
            forward_short(n, hop)
        hand_over(n, block(-hop))

    def handed_over(n):
        wait(b_all.at[0, pl.ds(0, Z_N), :, lanes_of(n)], dr_sem.at[n])

    def dot(a, b):
        return jnp.dot(a.reshape(-1, cols), b.reshape(cols, -1), preferred_element_type=jnp.float32)

    def out_copy(src, q, first, size, slot):
        return pltpu.make_async_copy(src, c_hbm.at[:, :, q, :, pl.ds(pl.multiple_of(first, size), size)],
                                     out_sem.at[slot])

    def sum_stage(n, g, q, m, lanes, first, size, when, reuse, old):
        slot = n % SLOTS
        keep = rest if isinstance(lanes, slice) else pl.ds(0, narrow)
        qi = 0 if isinstance(q, slice) else q

        def pass_on(src, ssem):
            for d in range(2):
                send(src.at[d], crecv.at[m, g, d, :, q, :, lanes], ssem, cr_sem.at[n, g, qi], at_x(1 - 2 * d))

        def arrived():
            wait(crecv.at[m, g - 1, :, :, q, :, lanes], cr_sem.at[n, g - 1, qi])

        def begin():
            reuse(lambda: wait(c0.at[slot, :, :, :, :, old], c0_sem.at[slot]))
            c0[slot, :, :, q, :, keep] = prod[:, :, q, :, keep]
            pass_on(c0.at[slot, :, :, q, :, keep], c0_sem.at[slot])

        def middle():
            arrived()
            crecv[m, g - 1, :, :, q, :, lanes] += prod[:, :, q, :, keep]
            pass_on(crecv.at[m, g - 1, :, :, q, :, lanes], cs_sem.at[m // 4])

        def end():
            arrived()
            reuse(lambda: wait(outst.at[slot, :, :, :, :, old], out_sem.at[slot]))
            total = crecv[m, g - 1, :, :, q, :, lanes] + prod[:, :, q, :, keep]
            outst[slot, :, :, q, :, keep] = total.astype(outst.dtype)
            out_copy(outst.at[slot, :, :, q, :, keep], q, first, size, slot).start()

        a = a_all[g, :, :, q]
        prod[:, :, q, :, keep] = dot(a, b_all[m, :, :, lanes]).reshape(a.shape[:-1] + (size,))
        when(g == 0, begin)
        when((g == 1) | (g == 2), middle)
        when(g == 3, end)

    def branch(cond, fn):
        pl.when(cond)(fn)

    def fixed(cond, fn):
        if cond:
            fn()

    def sum_loop(code, split, wide):
        n, g, q = code // 8, code // 2 % 4, code % 2
        if split:
            pl.when(n < SPLIT)(lambda: sum_stage(n, g, q, n, rest, n * width, width, branch, lambda fn: None, rest))
        if wide:
            pl.when(n >= SPLIT)(lambda: sum_stage(n, g, rest, n, rest, n * width, width, branch,
                                                  pl.when(n >= SLOTS), rest))

    def sum_narrow(n, g):
        m, half = chunk(n)
        old = rest if n - SLOTS < WIDE else pl.ds(0, narrow)
        sum_stage(n, g, rest, m, lanes_of(n), m * width + half * narrow, narrow, fixed, lambda fn: fn(), old)

    events = {S1: ev_s1, R1: ev_r1, S2: ev_s2, S2F: ev_s2f, R2: ev_r2, AG: ev_ag, FW: ev_fw,
              OWN: ev_own, LONG: ev_long, SHORT: ev_short}
    steps, before, complete, handed = [], [], set(), set()
    for kind, *args in ORDER:
        if kind != SUM:
            before.append((events[kind], args))
            continue
        n, g, q = args
        for r in (range(2) if q == ALL else (q,)):
            if (g, r) not in complete:
                complete.add((g, r))
                before.append((group_complete, (g, r)))
        if n not in handed:
            handed.add(n)
            before.append((handed_over, (n,)))
        if n >= WIDE:
            before.append((sum_narrow, (n, g)))
        else:
            steps.append((before, (n * 4 + g) * 2 + q % 2, q != ALL))
            before = []

    def run(todo):
        for fn, args in todo:
            fn(*args)

    def in_loop(first, last):
        part = steps[first:last]

        def body(k, carry):
            code = part[0][1]
            for i, (todo, this, _) in enumerate(part):
                code = jnp.where(k == first + i, this, code)
                if todo:
                    pl.when(k == first + i)(lambda: run(todo))
            sum_loop(code, any(s for _, _, s in part), any(not s for _, _, s in part))
            return carry

        lax.fori_loop(first, last, body, 0)

    for first in range(0, len(steps), LOOP):
        in_loop(first, min(first + LOOP, len(steps)))
    run(before)

    for i in range(BLOCKS // 4):
        wait(b_all.at[pl.ds(0, 4), pl.ds(0, 15)], zs_sem.at[i])
        wait(crecv.at[pl.ds(0, 4), pl.ds(0, 2)], cs_sem.at[i])
    wait(b_all.at[pl.ds(0, 5)], as_sem)
    for n in range(CHUNKS - SLOTS, CHUNKS):
        keep = rest if n < WIDE else pl.ds(0, narrow)
        wait(c0.at[n % SLOTS, :, :, :, :, keep], c0_sem.at[n % SLOTS])
        wait(outst.at[n % SLOTS, :, :, :, :, keep], out_sem.at[n % SLOTS])


def solution(mesh):
    def local_product(a_blk, b_blk):
        rows, cols = a_blk.shape
        width = cols // BLOCKS
        few = rows // 16
        dma = pltpu.SemaphoreType.DMA
        c_blk = pl.pallas_call(
            kernel,
            name="matmul_3d",
            out_shape=jax.ShapeDtypeStruct((2, 4, 2, few, cols), jnp.bfloat16),
            in_specs=[pl.BlockSpec(memory_space=pl.ANY)] * 2,
            out_specs=pl.BlockSpec(memory_space=pl.ANY),
            scratch_shapes=[
                pltpu.VMEM((2, 4, 2, few, cols), jnp.bfloat16),
                pltpu.VMEM((4, 2, 4, 2, few, cols), jnp.bfloat16),
                pltpu.VMEM((3, 2, 2, few, cols), jnp.bfloat16),
                pltpu.VMEM((2, 2, 2, few, cols // 2), jnp.bfloat16),
                pltpu.VMEM((2, 2, 2, few, cols // 2), jnp.bfloat16),
                pltpu.VMEM((BLOCKS, 2 * Z_N, rows, width), jnp.bfloat16),
                pltpu.VMEM((BLOCKS, 3, 2, 4, 2, few, width), jnp.float32),
                pltpu.VMEM((SLOTS, 2, 4, 2, few, width), jnp.float32),
                pltpu.VMEM((SLOTS, 2, 4, 2, few, width), jnp.bfloat16),
                pltpu.VMEM((2, 4, 2, few, width), jnp.float32),
                dma((3,)), dma((CHUNKS, 7)), dma((BLOCKS // 4,)), dma((CHUNKS,)),
                dma((4, 2, 2)), dma((2, 2, 2)), dma((2, 2, 2)), dma((3, 2, 2)), dma((4, 2, 2)), dma((4, 2)), dma,
                dma((CHUNKS, 3, 2 if SPLIT else 1)), dma((BLOCKS // 4,)), dma((SLOTS,)), dma((SLOTS,)),
            ],
            compiler_params=pltpu.CompilerParams(
                collective_id=0, has_side_effects=True, vmem_limit_bytes=67043328
            ),
        )(a_blk.reshape(2, 4, 2, few, cols), b_blk)
        return c_blk.reshape(rows, cols)

    block_spec = P(("row", "depth"), "col")
    return jax.shard_map(local_product, mesh=mesh, in_specs=(block_spec, block_spec), out_specs=block_spec, check_vma=False)
```

time: 502 us -> 200 us (0.40)
  waiting for transfers between devices: 325 us -> 0 us
  Pallas kernels: 0 us -> 197 us
  blocking collectives: 100 us -> 0 us
  matrix products: 43.5 us -> 0 us
  between operations: 13.1 us -> 0.01 us
  local copies, waits for them, and re-layouts: 15.5 us -> 3.13 us
    pallas_call x0 -> x1, Pallas kernels: none -> 197 us  [local_product(): pl.pallas_call(kernel, name='matmul_3d', out_shape=jax.ShapeDtypeStruct((...]
    reduce_scatter x1 -> x0, waiting for transfers between devices: 172 us -> none  [local_product(): c_part = lax.psum_scatter(part, 'row', scatter_dimension=0, tiled=True)]
    all_gather x2 -> x0, waiting for transfers between devices: 153 us -> none  [the longest x1 88.8 us: local_product(): a_rows = lax.all_gather(a_blk, 'col', axis=1, tiled=True)]
    all_to_all x1 -> x0, blocking collectives: 100 us -> none  [local_product(): a_k = lax.all_to_all(a_rows, 'row', split_axis=1, concat_axis=0, tiled=True)]
    dot_general x1 -> x0, matrix products: 43.5 us -> none  [local_product(): part = jnp.dot(a_k, b_full, preferred_element_type=jnp.float32)]
    all_to_all x1 -> x0, local copies, waits for them, and re-layouts: 11.5 us -> none  [local_product(): a_k = lax.all_to_all(a_rows, 'row', split_axis=1, concat_axis=0, tiled=True)]
  transfers between devices with their start and end apart: 3 -> 0, of which waited for: 3 -> 0; matrix products, arithmetic and copies ran while one was open for 2% -> 0% of each run, Pallas kernels for 0% -> 0%
where the time goes in v3:
time: 200 us
  Pallas kernels  197 us (98%)
  local copies, waits for them, and re-layouts  3.13 us (2%)
    pallas_call x1, Pallas kernels, local_product(): pl.pallas_call(kernel, name='matmul_3d', out_shape=jax.ShapeDtypeStruct((...  197 us

profile of v3, /device:TPU:1, one launch (start us, length us, event | category | flops | bytes accessed | tf_op | source)
XLA Modules:
  0.0 200.2 jit_solution(2633874372177333342)
XLA Ops:
  0.0 197.1 %matmul_3d.1 = bf16[2,4,2,16,4096]{4,3,2,1,0:T(8,128)(2,1)} custom-call(bf16[2,4,2,16,4096]{4,3,2,1,0:T(8,128)(2,1)} %bitcast.3, bf16[256,4096]{1,0:T(8,128)(2,1)} %b_hbm.1), custom_call_target="tpu_custom_call" | custom-call | tf_op jit(solution)/shard_map/matmul_3d/pallas_call | solution.py:342
  197.1 3.1 %copy.4 = bf16[256,4096]{1,0:T(8,128)(2,1)} copy(bf16[256,4096]{1,0:T(8,128)(2,1)} %bitcast.2) | data formatting | bytes 4194304

commit v4 on v3

--- a/solution.py
+++ b/solution.py
@@ -10,46 +10,17 @@
 BLOCKS = 16
 SLOTS = 4
 LOOP = 8
-S1, R1, S2, S2F, R2, AG, FW, OWN, LONG, SHORT, SUM = range(11)
 WIDE = 14
 SPLIT = 4
 ALL = 2
-ORDER = (
-    (7, 0), (0, 0, 0), (7, 1), (0, 0, 1), (7, 2), (1, 0, 0, 1), (1, 0, 0, 0), (0, 1, 0), (7, 3), (1, 0, 1, 1),
-    (9, 1, 1), (8, 1, 1), (2, 0, 0), (1, 0, 1, 0), (0, 1, 1), (8, 0, 1), (9, 3, 1), (8, 2, 1), (9, 2, 1), (2, 0, 1),
-    (9, 1, 2), (1, 1, 0, 0), (1, 1, 0, 1), (9, 0, 1), (5, 0, 0, 1), (8, 0, 2), (5, 0, 0, 0), (1, 1, 1, 1),
-    (1, 1, 1, 0), (8, 1, 2), (3, 1, 0), (2, 1, 0), (9, 3, 2), (8, 3, 1), (5, 0, 1, 1), (3, 0, 0), (8, 2, 2),
-    (6, 0, 0, 1), (5, 0, 1, 0), (4, 1, 0, 0), (7, 4), (4, 1, 0, 1), (3, 1, 1), (8, 3, 2), (8, 2, 3), (9, 1, 3),
-    (9, 2, 2), (5, 1, 0, 1), (8, 0, 3), (3, 0, 1), (6, 0, 1, 1), (4, 0, 0, 1), (9, 0, 2), (8, 1, 3), (8, 4, 1),
-    (4, 1, 1, 1), (8, 3, 3), (4, 0, 0, 0), (6, 0, 0, 0), (4, 0, 1, 0), (4, 1, 1, 0), (2, 1, 1), (6, 0, 1, 0),
-    (4, 0, 1, 1), (5, 1, 0, 0), (7, 5), (6, 1, 0, 1), (8, 0, 4), (8, 2, 4), (9, 3, 3), (9, 0, 3), (9, 2, 3),
-    (10, 0, 0, 0), (8, 1, 4), (5, 1, 1, 1), (9, 4, 1), (10, 2, 0, 0), (8, 4, 2), (10, 2, 0, 1), (10, 1, 0, 0),
-    (6, 1, 0, 0), (5, 1, 1, 0), (7, 6), (8, 3, 4), (10, 3, 0, 1), (5, 2, 0, 0), (10, 3, 0, 0), (9, 4, 2),
-    (10, 0, 0, 1), (8, 5, 1), (8, 4, 3), (10, 2, 1, 0), (8, 6, 1), (5, 2, 0, 1), (10, 0, 1, 0), (9, 5, 1),
-    (10, 1, 0, 1), (10, 1, 1, 0), (6, 1, 1, 1), (6, 1, 1, 0), (9, 6, 1), (8, 5, 2), (10, 3, 1, 0), (8, 4, 4),
-    (5, 2, 1, 0), (6, 2, 0, 0), (7, 7), (9, 4, 3), (10, 4, 0, 2), (9, 5, 2), (8, 6, 2), (10, 3, 1, 1), (5, 2, 1, 1),
-    (10, 1, 1, 1), (8, 5, 3), (9, 6, 2), (10, 2, 1, 1), (7, 8), (6, 2, 0, 1), (6, 2, 1, 0), (10, 0, 1, 1),
-    (10, 4, 1, 2), (9, 5, 3), (8, 7, 1), (8, 6, 3), (6, 2, 1, 1), (5, 3, 1, 0), (8, 5, 4), (10, 2, 2, 0),
-    (10, 5, 0, 2), (7, 9), (10, 3, 2, 1), (10, 4, 2, 2), (9, 6, 3), (9, 7, 1), (8, 8, 1), (5, 3, 0, 0), (8, 7, 2),
-    (5, 3, 1, 1), (10, 2, 2, 1), (8, 6, 4), (8, 9, 1), (10, 6, 0, 2), (7, 10), (10, 0, 2, 1), (8, 8, 2),
-    (10, 5, 1, 2), (6, 3, 0, 0), (10, 1, 2, 1), (8, 7, 3), (5, 3, 0, 1), (9, 8, 1), (8, 9, 2), (10, 6, 1, 2),
-    (9, 7, 2), (6, 3, 1, 1), (6, 3, 0, 1), (8, 8, 3), (7, 11), (10, 1, 2, 0), (10, 5, 2, 2), (6, 3, 1, 0), (9, 9, 1),
-    (10, 0, 2, 0), (8, 7, 4), (8, 9, 3), (10, 3, 2, 0), (9, 7, 3), (9, 8, 2), (9, 10, 1), (10, 7, 0, 2), (8, 10, 1),
-    (9, 9, 2), (10, 6, 2, 2), (8, 8, 4), (8, 11, 1), (9, 8, 3), (10, 8, 0, 2), (9, 11, 1), (10, 7, 1, 2), (8, 10, 2),
-    (10, 0, 3, 0), (9, 10, 2), (8, 9, 4), (7, 12), (9, 9, 3), (10, 9, 0, 2), (10, 0, 3, 1), (8, 11, 2), (10, 8, 1, 2),
-    (8, 10, 3), (8, 12, 1), (10, 7, 2, 2), (9, 12, 1), (8, 11, 3), (9, 10, 3), (9, 11, 2), (10, 9, 1, 2), (8, 10, 4),
-    (7, 13), (10, 1, 3, 0), (10, 8, 2, 2), (8, 12, 2), (9, 12, 2), (7, 14), (10, 10, 0, 2), (10, 1, 3, 1),
-    (10, 9, 2, 2), (8, 11, 4), (9, 11, 3), (8, 12, 3), (10, 11, 0, 2), (8, 13, 1), (10, 2, 3, 0), (10, 2, 3, 1),
-    (9, 12, 3), (7, 15), (9, 14, 1), (10, 10, 1, 2), (9, 13, 1), (8, 12, 4), (7, 16), (10, 12, 0, 2), (10, 3, 3, 0),
-    (8, 13, 2), (10, 11, 1, 2), (8, 16, 1), (8, 14, 1), (7, 17), (10, 3, 3, 1), (9, 13, 2), (8, 15, 1),
-    (10, 10, 2, 2), (10, 4, 3, 2), (10, 12, 1, 2), (8, 13, 3), (8, 14, 2), (10, 11, 2, 2), (8, 16, 2), (9, 15, 1),
-    (9, 14, 2), (9, 13, 3), (8, 13, 4), (8, 17, 1), (8, 15, 2), (9, 16, 1), (8, 14, 3), (10, 13, 0, 2),
-    (10, 12, 2, 2), (8, 16, 3), (8, 17, 2), (8, 15, 3), (9, 15, 2), (9, 17, 1), (9, 16, 2), (9, 14, 3), (8, 14, 4),
-    (10, 14, 0, 2), (8, 17, 3), (10, 13, 1, 2), (10, 5, 3, 2), (8, 15, 4), (9, 15, 3), (8, 16, 4), (9, 17, 2),
-    (9, 16, 3), (10, 15, 0, 2), (10, 16, 0, 2), (10, 14, 1, 2), (9, 17, 3), (8, 17, 4), (10, 17, 0, 2),
-    (10, 15, 1, 2), (10, 6, 3, 2), (10, 16, 1, 2), (10, 13, 2, 2), (10, 17, 1, 2), (10, 7, 3, 2), (10, 14, 2, 2),
-    (10, 8, 3, 2), (10, 9, 3, 2), (10, 15, 2, 2), (10, 10, 3, 2), (10, 16, 2, 2), (10, 17, 2, 2), (10, 11, 3, 2),
-    (10, 12, 3, 2), (10, 13, 3, 2), (10, 14, 3, 2), (10, 15, 3, 2), (10, 16, 3, 2), (10, 17, 3, 2),
+Z_SEMS, C_SEMS = 5, 7
+
+PROGRAM = (
+    "iaaiajfijbfbakjgibcflncmkkllbfjacdndomgcgmhlonodbamheheofkgn",
+    "odppcetatpotebohpgtdobfnqqnfachuqeqopcguauuodagbqoonrrrndrhv",
+    "ebpfvvcoeobhcpgqdarcfhsoqedfagbpfrodergavhpbqehcgfspqcbhrdgw",
+    "dqrfceawsshpwaerdgbpqfaebfahsacpgbqfsbrdqwccrfbghsecfsdpdrgh",
+    "gcdeepqdghheppsqehspqrssqqrsrrrsssss",
 )
 
 
@@ -60,9 +31,9 @@
 CHUNKS = WIDE + 2 * (BLOCKS - WIDE)
 
 
-def kernel(a_hbm, b_hbm, c_hbm, a_own, a_all, s1, rl1, rl2, b_all, crecv, c0, outst, prod,
+def kernel(a_hbm, b_hbm, c_out, a_own, a_all, s1, rl1, rl2, b_all, crecv, c0, prod,
            ld_sem, zr_sem, zs_sem, dr_sem, s1_sem, r1_sem, r2_sem, s2_sem, ag_sem, fw_sem, as_sem,
-           cr_sem, cs_sem, c0_sem, out_sem):
+           cr_sem, cs_sem, c0_sem):
     row, y, z = lax.axis_index("row"), lax.axis_index("col"), lax.axis_index("depth")
     x, c = row // 2, row % 2
     width = b_all.shape[3]
@@ -188,11 +159,11 @@
 
     def forward_long(n, hop):
         p = piece(n, block(hop))
-        send(p, p, zs_sem.at[chunk(n)[0] // 4], zr_sem.at[n, hop], z_long)
+        send(p, p, zs_sem.at[chunk(n)[0] // 4], zr_sem.at[n % Z_SEMS, hop], z_long)
 
     def forward_short(n, hop):
         p = piece(n, block(-hop))
-        send(p, p, zs_sem.at[chunk(n)[0] // 4], zr_sem.at[n, 4 + hop], z_short)
+        send(p, p, zs_sem.at[chunk(n)[0] // 4], zr_sem.at[n % Z_SEMS, 4 + hop], z_short)
 
     def ev_own(n):
         if n == 0:
@@ -204,13 +175,13 @@
         hand_over(n, block(0))
 
     def ev_long(n, hop):
-        wait(piece(n, block(hop)), zr_sem.at[n, hop - 1])
+        wait(piece(n, block(hop)), zr_sem.at[n % Z_SEMS, hop - 1])
         if hop < 4:
             forward_long(n, hop)
         hand_over(n, block(hop))
 
     def ev_short(n, hop):
-        wait(piece(n, block(-hop)), zr_sem.at[n, 4 + hop - 1])
+        wait(piece(n, block(-hop)), zr_sem.at[n % Z_SEMS, 4 + hop - 1])
         if hop < 3:
             forward_short(n, hop)
         hand_over(n, block(-hop))
@@ -221,21 +192,20 @@
     def dot(a, b):
         return jnp.dot(a.reshape(-1, cols), b.reshape(cols, -1), preferred_element_type=jnp.float32)
 
-    def out_copy(src, q, first, size, slot):
-        return pltpu.make_async_copy(src, c_hbm.at[:, :, q, :, pl.ds(pl.multiple_of(first, size), size)],
-                                     out_sem.at[slot])
+    def sum_sem(n, q):
+        return 2 * SPLIT + (n - SPLIT) % C_SEMS if isinstance(q, slice) else 2 * n + q
 
     def sum_stage(n, g, q, m, lanes, first, size, when, reuse, old):
         slot = n % SLOTS
         keep = rest if isinstance(lanes, slice) else pl.ds(0, narrow)
-        qi = 0 if isinstance(q, slice) else q
+        arrivals = sum_sem(n, q)
 
         def pass_on(src, ssem):
             for d in range(2):
-                send(src.at[d], crecv.at[m, g, d, :, q, :, lanes], ssem, cr_sem.at[n, g, qi], at_x(1 - 2 * d))
+                send(src.at[d], crecv.at[m, g, d, :, q, :, lanes], ssem, cr_sem.at[arrivals, g], at_x(1 - 2 * d))
 
         def arrived():
-            wait(crecv.at[m, g - 1, :, :, q, :, lanes], cr_sem.at[n, g - 1, qi])
+            wait(crecv.at[m, g - 1, :, :, q, :, lanes], cr_sem.at[arrivals, g - 1])
 
         def begin():
             reuse(lambda: wait(c0.at[slot, :, :, :, :, old], c0_sem.at[slot]))
@@ -249,10 +219,8 @@
 
         def end():
             arrived()
-            reuse(lambda: wait(outst.at[slot, :, :, :, :, old], out_sem.at[slot]))
             total = crecv[m, g - 1, :, :, q, :, lanes] + prod[:, :, q, :, keep]
-            outst[slot, :, :, q, :, keep] = total.astype(outst.dtype)
-            out_copy(outst.at[slot, :, :, q, :, keep], q, first, size, slot).start()
+            c_out[:, :, q, :, pl.ds(pl.multiple_of(first, size), size)] = total.astype(c_out.dtype)
 
         a = a_all[g, :, :, q]
         prod[:, :, q, :, keep] = dot(a, b_all[m, :, :, lanes]).reshape(a.shape[:-1] + (size,))
@@ -280,12 +248,37 @@
         old = rest if n - SLOTS < WIDE else pl.ds(0, narrow)
         sum_stage(n, g, rest, m, lanes_of(n), m * width + half * narrow, narrow, fixed, lambda fn: fn(), old)
 
-    events = {S1: ev_s1, R1: ev_r1, S2: ev_s2, S2F: ev_s2f, R2: ev_r2, AG: ev_ag, FW: ev_fw,
-              OWN: ev_own, LONG: ev_long, SHORT: ev_short}
+    def both(fn):
+        def two(*args):
+            fn(*args, 0)
+            fn(*args, 1)
+        return two
+
+    chunks = range(CHUNKS)
+    queues = {"a": [(ev_own, (n,)) for n in chunks]}
+    for hop in range(1, 5):
+        queues["abcde"[hop]] = [(ev_long, (n, hop)) for n in chunks]
+    for hop in range(1, 4):
+        queues["efgh"[hop]] = [(ev_short, (n, hop)) for n in chunks]
+    by_half = [(o, r) for o in range(2) for r in range(2)]
+    by_row = [(o, r) for r in range(2) for o in range(2)]
+    queues["i"] = [(ev_s1, p) for p in by_half]
+    queues["j"] = [(both(ev_r1), p) for p in by_half]
+    queues["k"] = [(ev_s2, p) for p in by_half]
+    queues["l"] = [(ev_s2f, p) for p in by_row]
+    queues["m"] = [(both(ev_r2), p) for p in by_row]
+    groups = [(g, r) for g in range(4) for r in range(2)]
+    queues["n"] = [(both(ev_ag), p) for p in groups]
+    queues["o"] = [(ev_fw, p + (d,)) for p in groups for d in range(2)]
+    for g in range(4):
+        queues["pqrs"[g]] = [(None, (n, g, 0 if n < SPLIT else ALL)) for n in chunks]
+        queues["tuvw"[g]] = [(None, (n, g, 1)) for n in range(SPLIT)]
+
     steps, before, complete, handed = [], [], set(), set()
-    for kind, *args in ORDER:
-        if kind != SUM:
-            before.append((events[kind], args))
+    for letter in "".join(PROGRAM):
+        fn, args = queues[letter].pop(0)
+        if fn is not None:
+            before.append((fn, args))
             continue
         n, g, q = args
         for r in (range(2) if q == ALL else (q,)):
@@ -330,7 +323,6 @@
     for n in range(CHUNKS - SLOTS, CHUNKS):
         keep = rest if n < WIDE else pl.ds(0, narrow)
         wait(c0.at[n % SLOTS, :, :, :, :, keep], c0_sem.at[n % SLOTS])
-        wait(outst.at[n % SLOTS, :, :, :, :, keep], out_sem.at[n % SLOTS])
 
 
 def solution(mesh):
@@ -342,9 +334,9 @@
         c_blk = pl.pallas_call(
             kernel,
             name="matmul_3d",
-            out_shape=jax.ShapeDtypeStruct((2, 4, 2, few, cols), jnp.bfloat16),
+            out_shape=pltpu.VMEM((2, 4, 2, few, cols), jnp.bfloat16),
             in_specs=[pl.BlockSpec(memory_space=pl.ANY)] * 2,
-            out_specs=pl.BlockSpec(memory_space=pl.ANY),
+            out_specs=pl.BlockSpec(memory_space=pltpu.VMEM),
             scratch_shapes=[
                 pltpu.VMEM((2, 4, 2, few, cols), jnp.bfloat16),
                 pltpu.VMEM((4, 2, 4, 2, few, cols), jnp.bfloat16),
@@ -354,14 +346,13 @@
                 pltpu.VMEM((BLOCKS, 2 * Z_N, rows, width), jnp.bfloat16),
                 pltpu.VMEM((BLOCKS, 3, 2, 4, 2, few, width), jnp.float32),
                 pltpu.VMEM((SLOTS, 2, 4, 2, few, width), jnp.float32),
-                pltpu.VMEM((SLOTS, 2, 4, 2, few, width), jnp.bfloat16),
                 pltpu.VMEM((2, 4, 2, few, width), jnp.float32),
-                dma((3,)), dma((CHUNKS, 7)), dma((BLOCKS // 4,)), dma((CHUNKS,)),
+                dma((3,)), dma((Z_SEMS, 7)), dma((BLOCKS // 4,)), dma((CHUNKS,)),
                 dma((4, 2, 2)), dma((2, 2, 2)), dma((2, 2, 2)), dma((3, 2, 2)), dma((4, 2, 2)), dma((4, 2)), dma,
-                dma((CHUNKS, 3, 2 if SPLIT else 1)), dma((BLOCKS // 4,)), dma((SLOTS,)), dma((SLOTS,)),
+                dma((2 * SPLIT + C_SEMS, 3)), dma((BLOCKS // 4,)), dma((SLOTS,)),
             ],
             compiler_params=pltpu.CompilerParams(
-                collective_id=0, has_side_effects=True, vmem_limit_bytes=67043328
+                collective_id=0, has_side_effects=True, vmem_limit_bytes=61 * 1024 * 1024
             ),
         )(a_blk.reshape(2, 4, 2, few, cols), b_blk)
         return c_blk.reshape(rows, cols)

time: 200 us -> 196 us (0.980)
  Pallas kernels: 197 us -> 195 us
    pallas_call x1, Pallas kernels: 197 us -> 195 us  [local_product(): pl.pallas_call(kernel, name='matmul_3d', out_shape=pltpu.VMEM((2, 4, 2, f...]
where the time goes in v4:
time: 196 us
  Pallas kernels  195 us (99%)
    pallas_call x1, Pallas kernels, local_product(): pl.pallas_call(kernel, name='matmul_3d', out_shape=pltpu.VMEM((2, 4, 2, f...  195 us

profile of v4, /device:TPU:1, one launch (start us, length us, event | category | flops | bytes accessed | tf_op | source)
XLA Modules:
  0.0 196.3 jit_solution(16189994155306948950)
XLA Ops:
  0.0 194.9 %matmul_3d.1 = bf16[2,4,2,16,4096]{4,3,2,1,0:T(8,128)(2,1)S(1)} custom-call(bf16[2,4,2,16,4096]{4,3,2,1,0:T(8,128)(2,1)} %bitcast.3, bf16[256,4096]{1,0:T(8,128)(2,1)} %b_hbm.1), custom_call_target="tpu_custom_call" | custom-call | tf_op jit(solution)/shard_map/matmul_3d/pallas_call | solution.py:334
  195.0 1.3 copy.4

commit v5 on v4

--- a/solution.py
+++ b/solution.py
@@ -8,19 +8,19 @@
 MESH = pl.DeviceIdType.MESH
 X_N, Y_N, Z_N = 4, 4, 8
 BLOCKS = 16
-SLOTS = 4
+SLOTS = 8
 LOOP = 8
 WIDE = 14
-SPLIT = 4
+SPLIT = 6
 ALL = 2
-Z_SEMS, C_SEMS = 5, 7
+Z_SEMS, C_SEMS = 6, 6
 
 PROGRAM = (
-    "iaaiajfijbfbakjgibcflncmkkllbfjacdndomgcgmhlonodbamheheofkgn",
-    "odppcetatpotebohpgtdobfnqqnfachuqeqopcguauuodagbqoonrrrndrhv",
-    "ebpfvvcoeobhcpgqdarcfhsoqedfagbpfrodergavhpbqehcgfspqcbhrdgw",
-    "dqrfceawsshpwaerdgbpqfaebfahsacpgbqfsbrdqwccrfbghsecfsdpdrgh",
-    "gcdeepqdghheppsqehspqrssqqrsrrrsssss",
+    "aaijabaibkiabjcljfnaifkklcgjdnbbmoomchffclneglkodmdmgofdgopa",
+    "ehcoehpnttnegtbphqdopaqbfoqchetnqatobpuufguuoboqcogudfrcrcav",
+    "nvvdhrvgeprndrdtoohfeaqvfpehbgufrebpacqvchgqoaprdssdgbsohreb",
+    "qfhescpawpgfdraswbcqehqgbpafswrdrcscwhaqewafgdbpbfdswrghebcq",
+    "fcfghepcsdpggrddhesqshheqpepprqsqqrrsrsrssss",
 )
 
 
@@ -262,9 +262,9 @@
         queues["efgh"[hop]] = [(ev_short, (n, hop)) for n in chunks]
     by_half = [(o, r) for o in range(2) for r in range(2)]
     by_row = [(o, r) for r in range(2) for o in range(2)]
-    queues["i"] = [(ev_s1, p) for p in by_half]
-    queues["j"] = [(both(ev_r1), p) for p in by_half]
-    queues["k"] = [(ev_s2, p) for p in by_half]
+    queues["i"] = [(ev_s1, p) for p in by_row]
+    queues["j"] = [(both(ev_r1), p) for p in by_row]
+    queues["k"] = [(ev_s2, p) for p in by_row]
     queues["l"] = [(ev_s2f, p) for p in by_row]
     queues["m"] = [(both(ev_r2), p) for p in by_row]
     groups = [(g, r) for g in range(4) for r in range(2)]

time: 196 us -> 196 us (level)
  no operation moved by 1% of the time
where the time goes in v5:
time: 196 us
  Pallas kernels  194 us (99%)
    pallas_call x1, Pallas kernels, local_product(): pl.pallas_call(kernel, name='matmul_3d', out_shape=pltpu.VMEM((2, 4, 2, f...  194 us

profile of v5, /device:TPU:1, one launch (start us, length us, event | category | flops | bytes accessed | tf_op | source)
XLA Modules:
  0.0 195.7 jit_solution(17779560735846763953)
XLA Ops:
  0.0 194.4 %matmul_3d.1 = bf16[2,4,2,16,4096]{4,3,2,1,0:T(8,128)(2,1)S(1)} custom-call(bf16[2,4,2,16,4096]{4,3,2,1,0:T(8,128)(2,1)} %bitcast.3, bf16[256,4096]{1,0:T(8,128)(2,1)} %b_hbm.1), custom_call_target="tpu_custom_call" | custom-call | tf_op jit(solution)/shard_map/matmul_3d/pallas_call | solution.py:334
  194.4 1.3 copy.4

commit v6 on v4

--- a/solution.py
+++ b/solution.py
@@ -8,19 +8,19 @@
 MESH = pl.DeviceIdType.MESH
 X_N, Y_N, Z_N = 4, 4, 8
 BLOCKS = 16
-SLOTS = 4
+SLOTS = 8
 LOOP = 8
 WIDE = 14
 SPLIT = 4
 ALL = 2
-Z_SEMS, C_SEMS = 5, 7
+Z_SEMS, C_SEMS = 6, 6
 
 PROGRAM = (
-    "iaaiajfijbfbakjgibcflncmkkllbfjacdndomgcgmhlonodbamheheofkgn",
-    "odppcetatpotebohpgtdobfnqqnfachuqeqopcguauuodagbqoonrrrndrhv",
-    "ebpfvvcoeobhcpgqdarcfhsoqedfagbpfrodergavhpbqehcgfspqcbhrdgw",
-    "dqrfceawsshpwaerdgbpqfaebfahsacpgbqfsbrdqwccrfbghsecfsdpdrgh",
-    "gcdeepqdghheppsqehspqrssqqrsrrrsssss",
+    "aiaaijajibiabkbkffjcnlccabkmflfjdngglommldocdbnmoeoebkhgdogh",
+    "ppofeanhttcphfeqcqgtbootnpdgquduuncuhfeaqohaepopbogqdfornnfr",
+    "rhbcvarvqvcdvgegoboadfrephaprochsqebsfobgspsgqfdwrqccsheardd",
+    "pwgrahfebawpehqbcpbqgcdfrcsqdfrgaehagdpewharbsefhbpqfbcgpcss",
+    "cfqgddrdhgsehqserhspepprsqsqqrrrssss",
 )
 
 

time: 196 us -> 197 us (level)
  no operation moved by 1% of the time
where the time goes in v6:
time: 197 us
  Pallas kernels  195 us (99%)
    pallas_call x1, Pallas kernels, local_product(): pl.pallas_call(kernel, name='matmul_3d', out_shape=pltpu.VMEM((2, 4, 2, f...  195 us

profile of v6, /device:TPU:1, one launch (start us, length us, event | category | flops | bytes accessed | tf_op | source)
XLA Modules:
  0.0 196.7 jit_solution(17373927616796704645)
XLA Ops:
  0.0 195.4 %matmul_3d.1 = bf16[2,4,2,16,4096]{4,3,2,1,0:T(8,128)(2,1)S(1)} custom-call(bf16[2,4,2,16,4096]{4,3,2,1,0:T(8,128)(2,1)} %bitcast.3, bf16[256,4096]{1,0:T(8,128)(2,1)} %b_hbm.1), custom_call_target="tpu_custom_call" | custom-call | tf_op jit(solution)/shard_map/matmul_3d/pallas_call | solution.py:334
  195.4 1.3 copy.4

commit v7 on v5

--- a/solution.py
+++ b/solution.py
@@ -68,14 +68,20 @@
         return pltpu.make_async_copy(b_hbm.at[:, pl.ds(pl.multiple_of(m * width, width), width)],
                                      b_all.at[m, c * Z_N + z], ld_sem.at[sem])
 
-    a_load = pltpu.make_async_copy(a_hbm, a_own, ld_sem.at[2])
-    a_load.start()
+    def a_load(r):
+        return pltpu.make_async_copy(a_hbm.at[:, :, r], a_own.at[:, :, r], ld_sem.at[2 + r])
+
+    a_load(0).start()
     b_local(0, 0).start()
+    a_load(1).start()
     barrier = pltpu.get_barrier_semaphore()
     for dev in (at_x(1), at_x(-1), at_y(1), at_y(-1), z_long, z_short, partner):
         pl.semaphore_signal(barrier, inc=1, device_id=dev, device_id_type=MESH)
     lax.fori_loop(1, BLOCKS, lambda m, _: (b_local(m, 1).start(), 0)[1], 0)
 
+    def quarter_sem(e, o, r):
+        return s1_sem.at[(e + 1) % 2 * (2 - e // 2), o, r]
+
     def by_e(e, o, r, j, part, fn):
         col_part = rest if part is None else part_cols[part]
 
@@ -90,49 +96,56 @@
     for o in range(2):
         for r in range(2):
             by_e(e_own, o, r, 0, None, lambda dst: pltpu.make_async_copy(
-                a_hbm.at[(o + flip) % 2, 0, r], dst, s1_sem.at[e_own, o, r]).start())
+                a_hbm.at[(o + flip) % 2, 0, r], dst, quarter_sem(e_own, o, r)).start())
     pl.semaphore_wait(barrier, 7)
-    a_load.wait()
+    loaded = set()
 
     def ev_s1(o, r):
+        if r not in loaded:
+            loaded.add(r)
+            a_load(r).wait()
         h = (o + flip) % 2
-        send(a_own.at[h, 2, r, :, part_cols[0]], rl1.at[0, o, r], as_sem, r1_sem.at[0, o, r], at_y(1))
-        send(a_own.at[h, 2, r, :, part_cols[1]], rl1.at[1, o, r], as_sem, r1_sem.at[1, o, r], at_y(-1))
-        sem = s1_sem.at[e_own, o, r]
+        send(a_own.at[h, 2, r, :, part_cols[0]], rl1.at[0, o, r], as_sem, r1_sem.at[o, r], at_y(1))
+        send(a_own.at[h, 2, r, :, part_cols[1]], rl1.at[1, o, r], as_sem, r1_sem.at[o, r], at_y(-1))
+        sem = quarter_sem(e_own, o, r)
         by_e(e_own, o, r, 1, None, lambda dst: send(a_own.at[h, 1, r], dst, as_sem, sem, at_y(1)))
         by_e(e_own, o, r, 3, None, lambda dst: send(a_own.at[h, 3, r], dst, as_sem, sem, at_y(-1)))
 
-    def ev_r1(o, r, d):
-        dy = 1 - 2 * d
-        e = (y - dy - x + 2 * Y_N) % Y_N
-        wait(rl1.at[d, o, r], r1_sem.at[d, o, r])
-        by_e(e, o, r, 2, d, lambda dst: send(rl1.at[d, o, r], dst, as_sem, s1_sem.at[e, o, r], at_y(dy)))
+    def ev_r1(o, r):
+        wait(rl1.at[:, o, r], r1_sem.at[o, r])
+        for d, dy in ((0, 1), (1, -1)):
+            e = (y - dy - x + 2 * Y_N) % Y_N
+            by_e(e, o, r, 2, d, lambda dst: send(rl1.at[d, o, r], dst, as_sem, quarter_sem(e, o, r), at_y(dy)))
 
     def ev_s2(o, r):
-        wait(s1.at[0, o, r], s1_sem.at[1, o, r])
-        wait(s1.at[2, o, r], s1_sem.at[3, o, r])
+        wait(s1.at[pl.ds(0, 2), o, r], quarter_sem(1, o, r))
         g = 2 * o
         j = (y - x - 1 + 2 * Y_N) % Y_N
-        send(s1.at[0, o, r], a_all.at[g, o, j, r], as_sem, s2_sem.at[g, o, r], at_x(1))
+        send(s1.at[0, o, r], a_all.at[g, o, j, r], as_sem, s2_sem.at[g, r], at_x(1))
         j = (y - x + 1 + Y_N) % Y_N
-        send(s1.at[2, o, r], a_all.at[g, 1 - o, j, r], as_sem, s2_sem.at[g, 1 - o, r], at_x(-1))
+        send(s1.at[2, o, r], a_all.at[g, 1 - o, j, r], as_sem, s2_sem.at[g, r], at_x(-1))
 
     def ev_s2f(o, r):
-        wait(s1.at[1, o, r], s1_sem.at[2, o, r])
+        wait(s1.at[1, o, r], quarter_sem(2, o, r))
         for d in range(2):
-            send(s1.at[1, o, r, :, part_cols[d]], rl2.at[d, o, r], as_sem, r2_sem.at[d, o, r], at_x(1 - 2 * d))
-
-    def ev_r2(o, r, d):
-        dx = 1 - 2 * d
-        j = (y - x - dx + 2 * Y_N) % Y_N
-        wait(rl2.at[d, o, r], r2_sem.at[d, o, r])
-        send(rl2.at[d, o, r], a_all.at[1, o, j, r, :, part_cols[d]], as_sem, s2_sem.at[1, o, r], at_x(dx))
-
-    def ev_ag(g, r, d):
-        quarter = a_all.at[g, d, j_own, r]
-        wait(quarter, s1_sem.at[0, d, r] if g == 3 else s2_sem.at[g, d, r])
-        send(quarter, quarter, as_sem, ag_sem.at[g, d, r], at_y(1))
-        send(quarter, quarter, as_sem, ag_sem.at[g, d, r], at_y(-1))
+            send(s1.at[1, o, r, :, part_cols[d]], rl2.at[d, o, r], as_sem, r2_sem.at[o, r], at_x(1 - 2 * d))
+
+    def ev_r2(o, r):
+        wait(rl2.at[:, o, r], r2_sem.at[o, r])
+        for d, dx in ((0, 1), (1, -1)):
+            j = (y - x - dx + 2 * Y_N) % Y_N
+            send(rl2.at[d, o, r], a_all.at[1, o, j, r, :, part_cols[d]], as_sem, s2_sem.at[1, r], at_x(dx))
+
+    def ev_ag(g, r):
+        if g == 3:
+            for o in range(2):
+                wait(a_all.at[g, o, j_own, r], quarter_sem(0, o, r))
+        else:
+            wait(a_all.at[g, :, j_own, r], s2_sem.at[g, r])
+        for d in range(2):
+            quarter = a_all.at[g, d, j_own, r]
+            send(quarter, quarter, as_sem, ag_sem.at[g, d, r], at_y(1))
+            send(quarter, quarter, as_sem, ag_sem.at[g, d, r], at_y(-1))
 
     def ev_fw(g, r, d):
         wait(a_all.at[0, 0, 0], ag_sem.at[g, d, r])
@@ -247,12 +260,6 @@
         m, half = chunk(n)
         old = rest if n - SLOTS < WIDE else pl.ds(0, narrow)
         sum_stage(n, g, rest, m, lanes_of(n), m * width + half * narrow, narrow, fixed, lambda fn: fn(), old)
-
-    def both(fn):
-        def two(*args):
-            fn(*args, 0)
-            fn(*args, 1)
-        return two
 
     chunks = range(CHUNKS)
     queues = {"a": [(ev_own, (n,)) for n in chunks]}
@@ -263,12 +270,12 @@
     by_half = [(o, r) for o in range(2) for r in range(2)]
     by_row = [(o, r) for r in range(2) for o in range(2)]
     queues["i"] = [(ev_s1, p) for p in by_row]
-    queues["j"] = [(both(ev_r1), p) for p in by_row]
+    queues["j"] = [(ev_r1, p) for p in by_row]
     queues["k"] = [(ev_s2, p) for p in by_row]
     queues["l"] = [(ev_s2f, p) for p in by_row]
-    queues["m"] = [(both(ev_r2), p) for p in by_row]
+    queues["m"] = [(ev_r2, p) for p in by_row]
     groups = [(g, r) for g in range(4) for r in range(2)]
-    queues["n"] = [(both(ev_ag), p) for p in groups]
+    queues["n"] = [(ev_ag, p) for p in groups]
     queues["o"] = [(ev_fw, p + (d,)) for p in groups for d in range(2)]
     for g in range(4):
         queues["pqrs"[g]] = [(None, (n, g, 0 if n < SPLIT else ALL)) for n in chunks]
@@ -347,8 +354,8 @@
                 pltpu.VMEM((BLOCKS, 3, 2, 4, 2, few, width), jnp.float32),
                 pltpu.VMEM((SLOTS, 2, 4, 2, few, width), jnp.float32),
                 pltpu.VMEM((2, 4, 2, few, width), jnp.float32),
-                dma((3,)), dma((Z_SEMS, 7)), dma((BLOCKS // 4,)), dma((CHUNKS,)),
-                dma((4, 2, 2)), dma((2, 2, 2)), dma((2, 2, 2)), dma((3, 2, 2)), dma((4, 2, 2)), dma((4, 2)), dma,
+                dma((4,)), dma((Z_SEMS, 7)), dma((BLOCKS // 4,)), dma((CHUNKS,)),
+                dma((3, 2, 2)), dma((2, 2)), dma((2, 2)), dma((3, 2)), dma((4, 2, 2)), dma((4, 2)), dma,
                 dma((2 * SPLIT + C_SEMS, 3)), dma((BLOCKS // 4,)), dma((SLOTS,)),
             ],
             compiler_params=pltpu.CompilerParams(

time: 196 us -> 196 us (level)
  no operation moved by 1% of the time
where the time goes in v7:
time: 196 us
  Pallas kernels  194 us (99%)
    pallas_call x1, Pallas kernels, local_product(): pl.pallas_call(kernel, name='matmul_3d', out_shape=pltpu.VMEM((2, 4, 2, f...  194 us

profile of v7, /device:TPU:1, one launch (start us, length us, event | category | flops | bytes accessed | tf_op | source)
XLA Modules:
  0.0 195.6 jit_solution(14929511686510237659)
XLA Ops:
  0.0 194.3 %matmul_3d.1 = bf16[2,4,2,16,4096]{4,3,2,1,0:T(8,128)(2,1)S(1)} custom-call(bf16[2,4,2,16,4096]{4,3,2,1,0:T(8,128)(2,1)} %bitcast.3, bf16[256,4096]{1,0:T(8,128)(2,1)} %b_hbm.1), custom_call_target="tpu_custom_call" | custom-call | tf_op jit(solution)/shard_map/matmul_3d/pallas_call | solution.py:341
  194.3 1.3 copy.4

commit v8 on v7

--- a/solution.py
+++ b/solution.py
@@ -13,14 +13,14 @@
 WIDE = 14
 SPLIT = 6
 ALL = 2
-Z_SEMS, C_SEMS = 6, 6
+Z_SEMS, C_SEMS = 5, 5
 
 PROGRAM = (
-    "aaijabaibkiabjcljfnaifkklcgjdnbbmoomchffclneglkodmdmgofdgopa",
-    "ehcoehpnttnegtbphqdopaqbfoqchetnqatobpuufguuoboqcogudfrcrcav",
-    "nvvdhrvgeprndrdtoohfeaqvfpehbgufrebpacqvchgqoaprdssdgbsohreb",
-    "qfhescpawpgfdraswbcqehqgbpafswrdrcscwhaqewafgdbpbfdswrghebcq",
-    "fcfghepcsdpggrddhesqshheqpepprqsqqrrsrsrssss",
+    "aiaiaajfijbakjbiblkgcbknffjcdlnlohmamlcgmgoofeocmhnddkphbdnb",
+    "egftceptoaoehptcopogntfdqfqnbduhaqqegucopotguuoqfheobaunrpth",
+    "dvcavqovgueobnrdvpbsvchefsofracopgrqvdwwwbsgwrdwrasqhefrchws",
+    "easpbpgsdfrbfcqehqascpgdrarbhqgdesfafbcpsehrgaqbcpdsbardgffh",
+    "eqbccfhepscgpddrggdhqeheqehpspprqqqrsrrrssss",
 )
 
 

time: 196 us -> 194 us (0.990)
  no operation moved by 1% of the time
where the time goes in v8:
time: 194 us
  Pallas kernels  193 us (99%)
    pallas_call x1, Pallas kernels, local_product(): pl.pallas_call(kernel, name='matmul_3d', out_shape=pltpu.VMEM((2, 4, 2, f...  193 us

profile of v8, /device:TPU:1, one launch (start us, length us, event | category | flops | bytes accessed | tf_op | source)
XLA Modules:
  0.0 193.9 jit_solution(1212665127579773647)
XLA Ops:
  0.0 192.6 %matmul_3d.1 = bf16[2,4,2,16,4096]{4,3,2,1,0:T(8,128)(2,1)S(1)} custom-call(bf16[2,4,2,16,4096]{4,3,2,1,0:T(8,128)(2,1)} %bitcast.3, bf16[256,4096]{1,0:T(8,128)(2,1)} %b_hbm.1), custom_call_target="tpu_custom_call" | custom-call | tf_op jit(solution)/shard_map/matmul_3d/pallas_call | solution.py:341
  192.6 1.3 copy.4

commit v9 on v8

--- a/solution.py
+++ b/solution.py
@@ -13,14 +13,14 @@
 WIDE = 14
 SPLIT = 6
 ALL = 2
-Z_SEMS, C_SEMS = 5, 5
+Z_SEMS, C_SEMS = 6, 5
 
 PROGRAM = (
-    "aiaiaajfijbakjbiblkgcbknffjcdlnlohmamlcgmgoofeocmhnddkphbdnb",
-    "egftceptoaoehptcopogntfdqfqnbduhaqqegucopotguuoqfheobaunrpth",
-    "dvcavqovgueobnrdvpbsvchefsofracopgrqvdwwwbsgwrdwrasqhefrchws",
-    "easpbpgsdfrbfcqehqascpgdrarbhqgdesfafbcpsehrgaqbcpdsbardgffh",
-    "eqbccfhepscgpddrggdhqeheqehpspprqqqrsrrrssss",
+    "aiaiafbjfiajalgjkaikncjbbkgblmnchlmfclooddhcoodfmbnmgepdgetn",
+    "kobehptcfehapoctotpondgfqfnqaqdquehbugptgououfqcoebohnuarpdt",
+    "vcragohqeuobnvdpvbshafsroevfvoccpsqvbwgwwgfrdwdqawrwresharch",
+    "espsfpbgsrdqbcafhgqesprdacrhbegffqsdbpshcarecgaqdbpdasbrhgef",
+    "fcqefbhpcgsdgpcrdgqdhheehqeppsprqqqsrrrrssss",
 )
 
 

time: 194 us -> 194 us (level)
  no operation moved by 1% of the time
where the time goes in v9:
time: 194 us
  Pallas kernels  193 us (99%)
    pallas_call x1, Pallas kernels, local_product(): pl.pallas_call(kernel, name='matmul_3d', out_shape=pltpu.VMEM((2, 4, 2, f...  193 us

profile of v9, /device:TPU:1, one launch (start us, length us, event | category | flops | bytes accessed | tf_op | source)
XLA Modules:
  0.0 194.2 jit_solution(12308997984142527449)
XLA Ops:
  0.0 192.9 %matmul_3d.1 = bf16[2,4,2,16,4096]{4,3,2,1,0:T(8,128)(2,1)S(1)} custom-call(bf16[2,4,2,16,4096]{4,3,2,1,0:T(8,128)(2,1)} %bitcast.3, bf16[256,4096]{1,0:T(8,128)(2,1)} %b_hbm.1), custom_call_target="tpu_custom_call" | custom-call | tf_op jit(solution)/shard_map/matmul_3d/pallas_call | solution.py:341
  192.9 1.3 copy.4

commit v10 on v9

--- a/solution.py
+++ b/solution.py
@@ -10,17 +10,17 @@
 BLOCKS = 16
 SLOTS = 8
 LOOP = 8
-WIDE = 14
+WIDE = 15
 SPLIT = 6
 ALL = 2
-Z_SEMS, C_SEMS = 6, 5
+Z_SEMS, C_SEMS = 5, 3
 
 PROGRAM = (
-    "aiaiafbjfiajalgjkaikncjbbkgblmnchlmfclooddhcoodfmbnmgepdgetn",
-    "kobehptcfehapoctotpondgfqfnqaqdquehbugptgououfqcoebohnuarpdt",
-    "vcragohqeuobnvdpvbshafsroevfvoccpsqvbwgwwgfrdwdqawrwresharch",
-    "espsfpbgsrdqbcafhgqesprdacrhbegffqsdbpshcarecgaqdbpdasbrhgef",
-    "fcqefbhpcgsdgpcrdgqdhheehqeppsprqqqsrrrrssss",
+    "aiaiafjafiabjbkjiknbbjckllgclbnfdmmocofdcgnldgkmchhgemoefdoa",
+    "hpeophonpdttgeqnbqoapehtoftcapqqbootnndqgfuufcueubhurgdptaro",
+    "carooehorngpufqvbdsssoaqcshbvegaovrrpwwwdscfrsbvefhbqfgdspwv",
+    "craqehwgdvacpshrebgwqbdpfsccrhgeaqdpdshfrbeqagapfsbrhcebqfcg",
+    "pdcsdfrhgeqdgehpehprspqqsqrrrsss",
 )
 
 

time: 194 us -> 195 us (level)
  no operation moved by 1% of the time
where the time goes in v10:
time: 195 us
  Pallas kernels  194 us (99%)
    pallas_call x1, Pallas kernels, local_product(): pl.pallas_call(kernel, name='matmul_3d', out_shape=pltpu.VMEM((2, 4, 2, f...  194 us

profile of v10, /device:TPU:1, one launch (start us, length us, event | category | flops | bytes accessed | tf_op | source)
XLA Modules:
  0.0 195.1 jit_solution(10454260232421539918)
XLA Ops:
  0.0 193.8 %matmul_3d.1 = bf16[2,4,2,16,4096]{4,3,2,1,0:T(8,128)(2,1)S(1)} custom-call(bf16[2,4,2,16,4096]{4,3,2,1,0:T(8,128)(2,1)} %bitcast.3, bf16[256,4096]{1,0:T(8,128)(2,1)} %b_hbm.1), custom_call_target="tpu_custom_call" | custom-call | tf_op jit(solution)/shard_map/matmul_3d/pallas_call | solution.py:341
  193.8 1.3 copy.4

commit v11 on v10

--- a/solution.py
+++ b/solution.py
@@ -11,16 +11,16 @@
 SLOTS = 8
 LOOP = 8
 WIDE = 15
-SPLIT = 6
+SPLIT = 4
 ALL = 2
-Z_SEMS, C_SEMS = 5, 3
+Z_SEMS, C_SEMS = 4, 3
 
 PROGRAM = (
-    "aiaiafjafiabjbkjiknbbjckllgclbnfdmmocofdcgnldgkmchhgemoefdoa",
-    "hpeophonpdttgeqnbqoapehtoftcapqqbootnndqgfuufcueubhurgdptaro",
-    "carooehorngpufqvbdsssoaqcshbvegaovrrpwwwdscfrsbvefhbqfgdspwv",
-    "craqehwgdvacpshrebgwqbdpfsccrhgeaqdpdshfrbeqagapfsbrhcebqfcg",
-    "pdcsdfrhgeqdgehpehprspqqsqrrrsss",
+    "aiaaijbfbijfbjkfgcialgcnjckldbmndhohaomlldckmeoefbmgoendpfng",
+    "apthotgpkcotheabotopdfnqbqcuhfauneucqopdgqoagobuqonherdranbp",
+    "orfhfcvvoebqcrpodgvgofrarssssdhwweqwvcaepbhgssdpbawrhfqcecpg",
+    "sbqffrdqhdcgaersgephrdfsbpaaheqscpgqabrdbhbqfcrecfgpdsrgfdsc",
+    "ehqehgdpspherpqqsqrrrsss",
 )
 
 
@@ -269,9 +269,9 @@
         queues["efgh"[hop]] = [(ev_short, (n, hop)) for n in chunks]
     by_half = [(o, r) for o in range(2) for r in range(2)]
     by_row = [(o, r) for r in range(2) for o in range(2)]
-    queues["i"] = [(ev_s1, p) for p in by_row]
-    queues["j"] = [(ev_r1, p) for p in by_row]
-    queues["k"] = [(ev_s2, p) for p in by_row]
+    queues["i"] = [(ev_s1, p) for p in by_half]
+    queues["j"] = [(ev_r1, p) for p in by_half]
+    queues["k"] = [(ev_s2, p) for p in by_half]
     queues["l"] = [(ev_s2f, p) for p in by_row]
     queues["m"] = [(ev_r2, p) for p in by_row]
     groups = [(g, r) for g in range(4) for r in range(2)]

time: 195 us -> 194 us (level)
  no operation moved by 1% of the time
where the time goes in v11:
time: 194 us
  Pallas kernels  193 us (99%)
    pallas_call x1, Pallas kernels, local_product(): pl.pallas_call(kernel, name='matmul_3d', out_shape=pltpu.VMEM((2, 4, 2, f...  193 us

profile of v11, /device:TPU:1, one launch (start us, length us, event | category | flops | bytes accessed | tf_op | source)
XLA Modules:
  0.0 193.9 jit_solution(15623030545938750900)
XLA Ops:
  0.0 192.6 %matmul_3d.1 = bf16[2,4,2,16,4096]{4,3,2,1,0:T(8,128)(2,1)S(1)} custom-call(bf16[2,4,2,16,4096]{4,3,2,1,0:T(8,128)(2,1)} %bitcast.3, bf16[256,4096]{1,0:T(8,128)(2,1)} %b_hbm.1), custom_call_target="tpu_custom_call" | custom-call | tf_op jit(solution)/shard_map/matmul_3d/pallas_call | solution.py:341
  192.6 1.3 copy.4

commit v12 on v9

--- a/solution.py
+++ b/solution.py
@@ -13,14 +13,14 @@
 WIDE = 14
 SPLIT = 6
 ALL = 2
-Z_SEMS, C_SEMS = 6, 5
+Z_SEMS, C_SEMS = 4, 5
 
 PROGRAM = (
-    "aiaiafbjfiajalgjkaikncjbbkgblmnchlmfclooddhcoodfmbnmgepdgetn",
-    "kobehptcfehapoctotpondgfqfnqaqdquehbugptgououfqcoebohnuarpdt",
-    "vcragohqeuobnvdpvbshafsroevfvoccpsqvbwgwwgfrdwdqawrwresharch",
-    "espsfpbgsrdqbcafhgqesprdacrhbegffqsdbpshcarecgaqdbpdasbrhgef",
-    "fcqefbhpcgsdgpcrdgqdhheehqeppsprqqqsrrrrssss",
+    "aiaifjibfajakbcjlifgkcbklnbahjnddlmcomlgfooeamoncdhmgkbdtneh",
+    "ogpfepctbehopaotgdtopcnqbqffnqquehduaoptogeuguocqhfbounardhp",
+    "tvrcoagqbveourndpbssavvhesocvfcopfqvbfwwwwdrgqgwdrracwaehsre",
+    "hspsbpdsgfrbcaqaeqhspgdrcffrhqbebsdgapscrgaechfqdpbshdargfeb",
+    "cqeffbhpcgdpcrdsghgeqdqehheppprsqqqsrrrrssss",
 )
 
 

time: 194 us -> 195 us (level)
  no operation moved by 1% of the time
where the time goes in v12:
time: 195 us
  Pallas kernels  194 us (99%)
    pallas_call x1, Pallas kernels, local_product(): pl.pallas_call(kernel, name='matmul_3d', out_shape=pltpu.VMEM((2, 4, 2, f...  194 us

profile of v12, /device:TPU:1, one launch (start us, length us, event | category | flops | bytes accessed | tf_op | source)
XLA Modules:
  0.0 195.4 jit_solution(10604587424572752256)
XLA Ops:
  0.0 194.1 %matmul_3d.1 = bf16[2,4,2,16,4096]{4,3,2,1,0:T(8,128)(2,1)S(1)} custom-call(bf16[2,4,2,16,4096]{4,3,2,1,0:T(8,128)(2,1)} %bitcast.3, bf16[256,4096]{1,0:T(8,128)(2,1)} %b_hbm.1), custom_call_target="tpu_custom_call" | custom-call | tf_op jit(solution)/shard_map/matmul_3d/pallas_call | solution.py:341
  194.1 1.3 copy.4

commit v13 on v8

--- a/solution.py
+++ b/solution.py
@@ -10,17 +10,17 @@
 BLOCKS = 16
 SLOTS = 8
 LOOP = 8
-WIDE = 14
+WIDE = 13
 SPLIT = 6
 ALL = 2
 Z_SEMS, C_SEMS = 5, 5
 
 PROGRAM = (
-    "aiaiaajfijbakjbiblkgcbknffjcdlnlohmamlcgmgoofeocmhnddkphbdnb",
-    "egftceptoaoehptcopogntfdqfqnbduhaqqegucopotguuoqfheobaunrpth",
-    "dvcavqovgueobnrdvpbsvchefsofracopgrqvdwwwbsgwrdwrasqhefrchws",
-    "easpbpgsdfrbfcqehqascpgdrarbhqgdesfafbcpsehrgaqbcpdsbardgffh",
-    "eqbccfhepscgpddrggdhqeheqehpspprqqqrsrrrssss",
+    "aiaiabjiafjkbjflcaikbbnckmjdlcgnlfcdekfohdaommgolbgonemtdghp",
+    "noehbcptfahoetpoctonndpgqfqdfaquheqbuopgteguooucqfbahounhrpd",
+    "tvvcoagqueorndbvpbsafvsherrovfocpqcsbgwwwwdwrgsqdfahcvarhesr",
+    "ewpsgbpsfdrqbchqgeaasfpdrarhcbfebqbgsfpdsacgchrcfgeaqdbhpdds",
+    "garebcehffqhebpfcpgpdcsgrdgqheqhdheqpesprpqrsqqrsrrrssss",
 )
 
 

time: 194 us -> 195 us (level)
  no operation moved by 1% of the time
where the time goes in v13:
time: 195 us
  Pallas kernels  193 us (99%)
    pallas_call x1, Pallas kernels, local_product(): pl.pallas_call(kernel, name='matmul_3d', out_shape=pltpu.VMEM((2, 4, 2, f...  193 us

profile of v13, /device:TPU:1, one launch (start us, length us, event | category | flops | bytes accessed | tf_op | source)
XLA Modules:
  0.0 194.5 jit_solution(3105727007715429687)
XLA Ops:
  0.0 193.2 %matmul_3d.1 = bf16[2,4,2,16,4096]{4,3,2,1,0:T(8,128)(2,1)S(1)} custom-call(bf16[2,4,2,16,4096]{4,3,2,1,0:T(8,128)(2,1)} %bitcast.3, bf16[256,4096]{1,0:T(8,128)(2,1)} %b_hbm.1), custom_call_target="tpu_custom_call" | custom-call | tf_op jit(solution)/shard_map/matmul_3d/pallas_call | solution.py:341
  193.2 1.3 copy.4

commit v14 on v11

--- a/solution.py
+++ b/solution.py
@@ -16,11 +16,11 @@
 Z_SEMS, C_SEMS = 4, 3
 
 PROGRAM = (
-    "aiaaijbfbijfbjkfgcialgcnjckldbmndhohaomlldckmeoefbmgoendpfng",
-    "apthotgpkcotheabotopdfnqbqcuhfauneucqopdgqoagobuqonherdranbp",
-    "orfhfcvvoebqcrpodgvgofrarssssdhwweqwvcaepbhgssdpbawrhfqcecpg",
-    "sbqffrdqhdcgaersgephrdfsbpaaheqscpgqabrdbhbqfcrecfgpdsrgfdsc",
-    "ehqehgdpspherpqqsqrrrsss",
+    "aiiaabjfbiajkjgbifclnfkcljblgcnmmddchlamefkoonhkddoebmgegfpo",
+    "anophecothabttopgdtponbqfqcqfhunauecupudgqoaaoobqohegnrndrbp",
+    "vrvcffqoehbvcroopgrodgrssasdsfwwhwhcevqasepgsbwpdbraqehfccpq",
+    "bgfsdrfqdhcegrasegphdrsbfpaaheqscpqgarbdbhqfcfrecbgpdrdscgfh",
+    "seqhdegpspehrpqsqqrrrsss",
 )
 
 

time: 194 us -> 193 us (level)
  Pallas kernels: 193 us -> 191 us
where the time goes in v14:
time: 193 us
  Pallas kernels  191 us (99%)
    pallas_call x1, Pallas kernels, local_product(): pl.pallas_call(kernel, name='matmul_3d', out_shape=pltpu.VMEM((2, 4, 2, f...  191 us

profile of v14, /device:TPU:1, one launch (start us, length us, event | category | flops | bytes accessed | tf_op | source)
XLA Modules:
  0.0 192.7 jit_solution(8049591029754597952)
XLA Ops:
  0.0 191.4 %matmul_3d.1 = bf16[2,4,2,16,4096]{4,3,2,1,0:T(8,128)(2,1)S(1)} custom-call(bf16[2,4,2,16,4096]{4,3,2,1,0:T(8,128)(2,1)} %bitcast.3, bf16[256,4096]{1,0:T(8,128)(2,1)} %b_hbm.1), custom_call_target="tpu_custom_call" | custom-call | tf_op jit(solution)/shard_map/matmul_3d/pallas_call | solution.py:341
  191.4 1.3 copy.4

commit v15 on v14

--- a/solution.py
+++ b/solution.py
@@ -10,17 +10,17 @@
 BLOCKS = 16
 SLOTS = 8
 LOOP = 8
-WIDE = 15
+WIDE = 16
 SPLIT = 4
 ALL = 2
-Z_SEMS, C_SEMS = 4, 3
+Z_SEMS, C_SEMS = 5, 3
 
 PROGRAM = (
-    "aiiaabjfbiajkjgbifclnfkcljblgcnmmddchlamefkoonhkddoebmgegfpo",
-    "anophecothabttopgdtponbqfqcqfhunauecupudgqoaaoobqohegnrndrbp",
-    "vrvcffqoehbvcroopgrodgrssasdsfwwhwhcevqasepgsbwpdbraqehfccpq",
-    "bgfsdrfqdhcegrasegphdrsbfpaaheqscpqgarbdbhqfcfrecbgpdrdscgfh",
-    "seqhdegpspehrpqsqqrrrsss",
+    "aiaiabjiajbaicbjffklkcbjnlkgfdlmdnlmocfmchbomggoedeodnpgkfat",
+    "ancheohhpetbtootgppondbqfqqhcaeuungpudoucbfaoqheoqondpgfrfrc",
+    "vnbvoheaqoprdvgcovrbroaressgswdwwfwhcsqhasepgbsdpbrfhaqcecpq",
+    "gbfsdrqdchfregsapedhgraspbaehfqspqcbrgdcqfhebfrdgpsrcsehgqdp",
+    "hserpqsqrrss",
 )
 
 

time: 193 us -> 195 us (1.010)
  Pallas kernels: 191 us -> 193 us
    pallas_call x1, Pallas kernels: 191 us -> 193 us  [local_product(): pl.pallas_call(kernel, name='matmul_3d', out_shape=pltpu.VMEM((2, 4, 2, f...]
where the time goes in v15:
time: 195 us
  Pallas kernels  193 us (99%)
    pallas_call x1, Pallas kernels, local_product(): pl.pallas_call(kernel, name='matmul_3d', out_shape=pltpu.VMEM((2, 4, 2, f...  193 us

profile of v15, /device:TPU:1, one launch (start us, length us, event | category | flops | bytes accessed | tf_op | source)
XLA Modules:
  0.0 194.8 jit_solution(14449519471917493666)
XLA Ops:
  0.0 193.4 %matmul_3d.1 = bf16[2,4,2,16,4096]{4,3,2,1,0:T(8,128)(2,1)S(1)} custom-call(bf16[2,4,2,16,4096]{4,3,2,1,0:T(8,128)(2,1)} %bitcast.3, bf16[256,4096]{1,0:T(8,128)(2,1)} %b_hbm.1), custom_call_target="tpu_custom_call" | custom-call | tf_op jit(solution)/shard_map/matmul_3d/pallas_call | solution.py:341
  193.4 1.3 copy.4

commit v16 on v14

--- a/solution.py
+++ b/solution.py
@@ -16,11 +16,11 @@
 Z_SEMS, C_SEMS = 4, 3
 
 PROGRAM = (
-    "aiiaabjfbiajkjgbifclnfkcljblgcnmmddchlamefkoonhkddoebmgegfpo",
-    "anophecothabttopgdtponbqfqcqfhunauecupudgqoaaoobqohegnrndrbp",
-    "vrvcffqoehbvcroopgrodgrssasdsfwwhwhcevqasepgsbwpdbraqehfccpq",
-    "bgfsdrfqdhcegrasegphdrsbfpaaheqscpqgarbdbhqfcfrecbgpdrdscgfh",
-    "seqhdegpspehrpqsqqrrrsss",
+    "aiaiajbjibffcbijkkafgjnclcbdnlhdllamkmcogogfmdomekohnbdehgpt",
+    "feanohpctpebotaodpotgnfqbnqqcehfuaupdugoqoacnuobgqeoahrrpdno",
+    "rcrbhbvffeoqrcvvdpgoovfssdsgsrehawwcweqahpwgsbsdpbraqcehfcpq",
+    "bgfsrdqdfchregsaegprhdsbfpaaheqscpqgarbdbhqffrcecbgpdrdsgfch",
+    "seqehdgpspehrpqsqqrrrsss",
 )
 
 

time: 193 us -> 193 us (level)
  no operation moved by 1% of the time
where the time goes in v16:
time: 193 us
  Pallas kernels  191 us (99%)
    pallas_call x1, Pallas kernels, local_product(): pl.pallas_call(kernel, name='matmul_3d', out_shape=pltpu.VMEM((2, 4, 2, f...  191 us

profile of v16, /device:TPU:1, one launch (start us, length us, event | category | flops | bytes accessed | tf_op | source)
XLA Modules:
  0.0 192.8 jit_solution(1480282767010066780)
XLA Ops:
  0.0 191.5 %matmul_3d.1 = bf16[2,4,2,16,4096]{4,3,2,1,0:T(8,128)(2,1)S(1)} custom-call(bf16[2,4,2,16,4096]{4,3,2,1,0:T(8,128)(2,1)} %bitcast.3, bf16[256,4096]{1,0:T(8,128)(2,1)} %b_hbm.1), custom_call_target="tpu_custom_call" | custom-call | tf_op jit(solution)/shard_map/matmul_3d/pallas_call | solution.py:341
  191.5 1.3 copy.4

commit v17 on v16

--- a/solution.py
+++ b/solution.py
@@ -16,11 +16,11 @@
 Z_SEMS, C_SEMS = 4, 3
 
 PROGRAM = (
-    "aiaiajbjibffcbijkkafgjnclcbdnlhdllamkmcogogfmdomekohnbdehgpt",
-    "feanohpctpebotaodpotgnfqbnqqcehfuaupdugoqoacnuobgqeoahrrpdno",
-    "rcrbhbvffeoqrcvvdpgoovfssdsgsrehawwcweqahpwgsbsdpbraqcehfcpq",
-    "bgfsrdqdfchregsaegprhdsbfpaaheqscpqgarbdbhqffrcecbgpdrdsgfch",
-    "seqehdgpspehrpqsqqrrrsss",
+    "aiiajaafibfbjikbfcbjkgjlgnlalmlhcdknfcomcmomdhogeodbnpngedet",
+    "fhatkeohcpaoptobtdgponnbqfaqqhceuucopfqgduuaobaqoongdehrrnpb",
+    "rrcvbfqfehcovopgoodrvgcsdssrwhfawsqeashevpsbgpdbwwrfahceqcpq",
+    "bsgfdrfqhdecgrasgpehrdsbpfhaeqscapgbqadrhqbffcbrecgpdrcsgfds",
+    "heqdhegpspherpqsqqrrrsss",
 )
 
 

time: 193 us -> 194 us (level)
  no operation moved by 1% of the time
where the time goes in v17:
time: 194 us
  Pallas kernels  192 us (99%)
    pallas_call x1, Pallas kernels, local_product(): pl.pallas_call(kernel, name='matmul_3d', out_shape=pltpu.VMEM((2, 4, 2, f...  192 us

profile of v17, /device:TPU:1, one launch (start us, length us, event | category | flops | bytes accessed | tf_op | source)
XLA Modules:
  0.0 193.6 jit_solution(8575373999202525472)
XLA Ops:
  0.0 192.3 %matmul_3d.1 = bf16[2,4,2,16,4096]{4,3,2,1,0:T(8,128)(2,1)S(1)} custom-call(bf16[2,4,2,16,4096]{4,3,2,1,0:T(8,128)(2,1)} %bitcast.3, bf16[256,4096]{1,0:T(8,128)(2,1)} %b_hbm.1), custom_call_target="tpu_custom_call" | custom-call | tf_op jit(solution)/shard_map/matmul_3d/pallas_call | solution.py:341
  192.3 1.3 copy.4

commit v18 on v17

--- a/solution.py
+++ b/solution.py
@@ -13,14 +13,14 @@
 WIDE = 15
 SPLIT = 4
 ALL = 2
-Z_SEMS, C_SEMS = 4, 3
+Z_SEMS, C_SEMS = 5, 3
 
 PROGRAM = (
-    "aiiajaafibfbjikbfcbjkgjlgnlalmlhcdknfcomcmomdhogeodbnpngedet",
-    "fhatkeohcpaoptobtdgponnbqfaqqhceuucopfqgduuaobaqoongdehrrnpb",
-    "rrcvbfqfehcovopgoodrvgcsdssrwhfawsqeashevpsbgpdbwwrfahceqcpq",
-    "bsgfdrfqhdecgrasgpehrdsbpfhaeqscapgbqadrhqbffcbrecgpdrcsgfds",
-    "heqdhegpspherpqsqqrrrsss",
+    "aiaaifjibjafklibjfabkjbnccnglmlckdhmcfooglkobdgogndmhmedteaf",
+    "hcnpepeaothtoobppdontgffqnqcqbehuuaopudogucqbnaqhoegaorpnrrd",
+    "cbhrbqfeordofvpcovvovgfgssssedhwarscwqhwgepawbspdbrahefqccpq",
+    "bgfsdrdqcfrhgeseapghdrsbfpaheqsacpqgarbdhbqffrcecbsgpdrdcgfs",
+    "heqhedgpspherpqsqqrrrsss",
 )
 
 

time: 194 us -> 194 us (level)
  no operation moved by 1% of the time
where the time goes in v18:
time: 194 us
  Pallas kernels  192 us (99%)
    pallas_call x1, Pallas kernels, local_product(): pl.pallas_call(kernel, name='matmul_3d', out_shape=pltpu.VMEM((2, 4, 2, f...  192 us

profile of v18, /device:TPU:1, one launch (start us, length us, event | category | flops | bytes accessed | tf_op | source)
XLA Modules:
  0.0 193.6 jit_solution(10345544849741593567)
XLA Ops:
  0.0 192.3 %matmul_3d.1 = bf16[2,4,2,16,4096]{4,3,2,1,0:T(8,128)(2,1)S(1)} custom-call(bf16[2,4,2,16,4096]{4,3,2,1,0:T(8,128)(2,1)} %bitcast.3, bf16[256,4096]{1,0:T(8,128)(2,1)} %b_hbm.1), custom_call_target="tpu_custom_call" | custom-call | tf_op jit(solution)/shard_map/matmul_3d/pallas_call | solution.py:341
  192.3 1.3 copy.4

commit v19 on v18

--- a/solution.py
+++ b/solution.py
@@ -16,11 +16,11 @@
 Z_SEMS, C_SEMS = 5, 3
 
 PROGRAM = (
-    "aiaaifjibjafklibjfabkjbnccnglmlckdhmcfooglkobdgogndmhmedteaf",
-    "hcnpepeaothtoobppdontgffqnqcqbehuuaopudogucqbnaqhoegaorpnrrd",
-    "cbhrbqfeordofvpcovvovgfgssssedhwarscwqhwgepawbspdbrahefqccpq",
-    "bgfsdrdqcfrhgeseapghdrsbfpaheqsacpqgarbdhbqffrcecbsgpdrdcgfs",
-    "heqhedgpspherpqsqqrrrsss",
+    "aiaiaajibfjbkibfbjfalcknjlnccogdfmcgollmkmddgnoebmdegkhfeoha",
+    "nhcpphopteattoobtdogpfnqncqaqheuubogpdoauuqcobafnqherboprrrd",
+    "ngocofqbfcrehvvvdopvofggssdscsaawwrehseqwwdhpgspbbrahfqecpcq",
+    "sbgrdfdfcqhregsaepghrdsbpfaheqscapbgaqdrbhqffrcecbgpdsdrcgfh",
+    "seqehdgpspherpqsqqrrrsss",
 )
 
 

time: 194 us -> 194 us (level)
  no operation moved by 1% of the time
where the time goes in v19:
time: 194 us
  Pallas kernels  193 us (99%)
    pallas_call x1, Pallas kernels, local_product(): pl.pallas_call(kernel, name='matmul_3d', out_shape=pltpu.VMEM((2, 4, 2, f...  193 us

profile of v19, /device:TPU:1, one launch (start us, length us, event | category | flops | bytes accessed | tf_op | source)
XLA Modules:
  0.0 194.2 jit_solution(919011373950590970)
XLA Ops:
  0.0 192.8 %matmul_3d.1 = bf16[2,4,2,16,4096]{4,3,2,1,0:T(8,128)(2,1)S(1)} custom-call(bf16[2,4,2,16,4096]{4,3,2,1,0:T(8,128)(2,1)} %bitcast.3, bf16[256,4096]{1,0:T(8,128)(2,1)} %b_hbm.1), custom_call_target="tpu_custom_call" | custom-call | tf_op jit(solution)/shard_map/matmul_3d/pallas_call | solution.py:341
  192.8 1.3 copy.4
